TPU v7x, 32 devices: a whole 2x2x4 slice. The times are simulated.
32 devices in a mesh: gx: 8 (over z, y), gy: 4 (over x, core).
Axes of the slice: x: 2, y: 2, z: 4, core: 2. Of those that a mesh axis runs over, the one named last changes fastest.
Arguments:
- velocity_u: float32 [4, 1280, 1024], P(None, 'gy', 'gx'), may hold values from -6 to 6
- velocity_v: float32 [4, 1280, 1024], P(None, 'gy', 'gx'), may hold values from -6 to 6
- tracer: float32 [4, 1280, 1024], P(None, 'gy', 'gx'), may hold values from -6 to 6
- pressure_old: float32 [1280, 1024], P('gy', 'gx'), may hold values from -6 to 6
- depth: float32 [1280, 1024], P('gy', 'gx'), may hold values from 0.5 to 2
- helm: float32 [1280, 1024], P('gy', 'gx'), may hold values from 0.05 to 0.5
- land_mask: int32 [1280, 1024], P('gy', 'gx'), may hold values from 0 to 1, as said below
- clinic_map: int32 [32, 8], replicated, may hold values from 0 to 1, as said below
- tropic_map: int32 [32, 8], replicated, may hold values from -1 to 47, as said below
Outputs:
- velocity_u_new: float32 [4, 1280, 1024], P(None, 'gy', 'gx')
- velocity_v_new: float32 [4, 1280, 1024], P(None, 'gy', 'gx')
- tracer_new: float32 [4, 1280, 1024], P(None, 'gy', 'gx')
- pressure: float32 [1280, 1024], P('gy', 'gx')
Inputs may be any that keep to these rules, and one draw needn't show every extreme that they name: `land_mask`: rows 0 and 1279 are land; every column of a block whose tropic_map entry is -1 is land; every other block has an ocean column. `clinic_map`: 1 exactly on the blocks whose tropic_map entry is not -1. `tropic_map`: A quarter of the blocks of every device's clinic domain are -1. Another value t places the block in slot t % 6 of the device with gx index t // 6 and the gy index of the device that holds the block's rows; no slot is named twice. The blocks of one device's clinic domain place at most 1 block on any one device, and this bound is reached; every device receives at most 6 blocks, and this bound is reached.
All inputs are finite; a program needn't handle non-finite values.
Results may differ from a plain program's by a relative error of at most 0.00026.
Values sent between devices are 32-bit elements; how exact they have to be, the bound alone decides.
No kernel may reach another device: no remote copies, remote signals or barrier semaphores. Data moves between devices by JAX's collectives and lax.ppermute only.
A program may use at most 64 MiB of HBM per device.

v0:
```python
import jax
import jax.numpy as jnp
from jax import lax
from jax.sharding import PartitionSpec as P

BX = 128
BY = 40
ITERS = 4


step_time = 0.2
viscosity = 0.5
diffusivity = 0.5
vertical = 0.5
gravity = 1.0


def padded_2(cells, sides, width):
    for axis, dim in sides:
        count = lax.axis_size(axis)
        head = lax.slice_in_dim(cells, 0, width, axis=dim)
        tail = lax.slice_in_dim(cells, cells.shape[dim] - width, cells.shape[dim], axis=dim)
        cells = jnp.concatenate(
            [
                lax.ppermute(tail, axis, [(i, (i + 1) % count) for i in range(count)]),
                cells,
                lax.ppermute(head, axis, [((i + 1) % count, i) for i in range(count)]),
            ],
            axis=dim,
        )
    return cells


def beside_all(padded):
    centre = padded[..., 1:-1, 1:-1]
    return (
        centre,
        padded[..., 1:-1, 2:],
        padded[..., 1:-1, :-2],
        padded[..., 2:, 1:-1],
        padded[..., :-2, 1:-1],
    )


def faces(depths):
    centre, east_v, west_v, north_v, south_v = beside_all(depths)
    return (
        jnp.minimum(centre, east_v),
        jnp.minimum(centre, west_v),
        jnp.minimum(centre, north_v),
        jnp.minimum(centre, south_v),
    )


def diffuse(padded, coeffs):
    centre, east_v, west_v, north_v, south_v = beside_all(padded)
    face_e, face_w, face_n, face_s = coeffs
    return (
        face_e * (east_v - centre)
        + face_w * (west_v - centre)
        + face_n * (north_v - centre)
        + face_s * (south_v - centre)
    )


def mixing(field):
    diff = field[1:] - field[:-1]
    zero = jnp.zeros_like(field[:1])
    return jnp.concatenate([diff, zero], 0) - jnp.concatenate([zero, diff], 0)


def norm_total(residual, precond):
    return lax.psum(jnp.sum(residual * precond), ("gx", "gy"))


def conjugate(apply, rhs, start, diagonal):
    solution = start
    residual = rhs - apply(start)
    precond = residual / diagonal
    direction = precond
    rz_now = norm_total(residual, precond)
    for step in range(ITERS):
        image = apply(direction)
        alpha = rz_now / lax.psum(jnp.sum(direction * image), ("gx", "gy"))
        solution = solution + alpha * direction
        residual = residual - alpha * image
        if step + 1 < ITERS:
            precond = residual / diagonal
            rz_next = norm_total(residual, precond)
            direction = precond + rz_next / rz_now * direction
            rz_now = rz_next
    return solution


def on_device(
    velocity_u, velocity_v, tracer, pressure_old, depth, helm, land_mask, clinic_map, tropic_map
):
    f32 = jnp.float32
    levels, rows, cols = velocity_u.shape
    width_y = lax.axis_size("gy")
    col_dev = lax.axis_index("gx")
    row_dev = lax.axis_index("gy")
    per_y = rows // BY
    per_x = cols // BX
    total_rows = rows * width_y
    my_tropic = lax.dynamic_slice(tropic_map, (row_dev * per_y, col_dev * per_x), (per_y, per_x))
    my_clinic = lax.dynamic_slice(clinic_map, (row_dev * per_y, col_dev * per_x), (per_y, per_x))

    def spread(blockwise):
        return jnp.broadcast_to(blockwise[:, None, :, None], (per_y, BY, per_x, BX)).reshape(
            rows, cols
        )

    ocean = land_mask.astype(f32)
    domain = spread((my_tropic >= 0).astype(f32))
    active = spread(my_clinic.astype(f32))
    solve_mask = ocean * domain
    wet = depth * solve_mask
    stacked = jnp.concatenate([velocity_u, velocity_v, tracer, wet[None]], 0)
    padded = padded_2(stacked, (("gx", 2), ("gy", 1)), 2)
    u_pad = padded[:levels]
    v_pad = padded[levels : 2 * levels]
    wet_pad = padded[3 * levels]
    cycle_faces = faces(wet_pad)
    inner_faces = tuple((face[1:-1, 1:-1] for face in cycle_faces))
    latitude = ((row_dev * rows - 1 + jnp.arange(rows + 2)) % total_rows).astype(f32)
    coriolis = (0.2 + 0.6 * ((latitude + 0.5) / total_rows)).reshape(rows + 2, 1)
    u_cycle = u_pad[:, 1:-1, 1:-1]
    v_cycle = v_pad[:, 1:-1, 1:-1]
    u_star = u_cycle + step_time * (
        vertical * mixing(u_cycle) + viscosity * diffuse(u_pad, cycle_faces) + coriolis * v_cycle
    )
    v_star = v_cycle + step_time * (
        vertical * mixing(v_cycle) + viscosity * diffuse(v_pad, cycle_faces) - coriolis * u_cycle
    )
    tracer_pad = padded[2 * levels : 3 * levels, 1:-1, 1:-1]
    _, tracer_e, tracer_w, tracer_n, tracer_s = beside_all(tracer_pad)
    tracer_raw = tracer + step_time * (
        vertical * mixing(tracer)
        + diffusivity * diffuse(tracer_pad, inner_faces)
        - 0.5 * (velocity_u * (tracer_e - tracer_w) + velocity_v * (tracer_n - tracer_s))
    )
    thick = ((2 * jnp.arange(levels) + 1).astype(f32) / (levels * levels)).reshape(levels, 1, 1)
    wet_cycle = wet_pad[1:-1, 1:-1]
    east_flow = wet_cycle * jnp.sum(thick * u_star, 0)
    north_flow = wet_cycle * jnp.sum(thick * v_star, 0)
    forcing = solve_mask * (
        -(east_flow[1:-1, 1:-1] - east_flow[1:-1, :-2])
        - (north_flow[1:-1, 1:-1] - north_flow[:-2, 1:-1])
    )
    face_e, face_w, face_n, face_s = inner_faces
    diagonal = helm + face_e + face_w + face_n + face_s
    start = solve_mask * pressure_old

    def plane_pad(field):
        return padded_2(field, (("gx", 1), ("gy", 0)), 1)

    def apply_plane(field):
        _, east_v, west_v, north_v, south_v = beside_all(plane_pad(field))
        return (
            diagonal * field
            - face_e * east_v
            - face_w * west_v
            - face_n * north_v
            - face_s * south_v
        )

    pressure = conjugate(apply_plane, forcing, start, diagonal)
    _, east_p, _, north_p, _ = beside_all(plane_pad(pressure))
    grad_x = east_p - pressure
    grad_y = north_p - pressure
    keep_mask = active * ocean
    u_new = keep_mask * (u_star[:, 1:-1, 1:-1] - gravity * grad_x) + (1.0 - active) * velocity_u
    v_new = keep_mask * (v_star[:, 1:-1, 1:-1] - gravity * grad_y) + (1.0 - active) * velocity_v
    t_new = keep_mask * tracer_raw + (1.0 - active) * tracer
    return (u_new, v_new, t_new, pressure)


def solution(mesh):
    in_specs = (
        P(None, "gy", "gx"),
        P(None, "gy", "gx"),
        P(None, "gy", "gx"),
        P("gy", "gx"),
        P("gy", "gx"),
        P("gy", "gx"),
        P("gy", "gx"),
        P(),
        P(),
    )
    out_specs = (P(None, "gy", "gx"), P(None, "gy", "gx"), P(None, "gy", "gx"), P("gy", "gx"))
    return jax.shard_map(
        on_device, mesh=mesh, in_specs=in_specs, out_specs=out_specs, check_vma=False
    )
```

profile of v0, /device:TPU:0, one launch (start us, length us, event | category | flops | bytes accessed | tf_op | source)
XLA Modules:
  0.0 433.9 jit_solution(4842136148970560075)
XLA Ops:
  2.5 1.0 copy.36
  3.6 1.1 copy.37
  4.7 1.0 copy.47
  5.8 1.4 copy.38
  7.4 1.4 copy.40
  9.6 3.0 collective-permute-start
  12.6 3.1 collective-permute-start.1
  16.3 2.0 collective-permute-start.4
  19.8 1.3 pad_maximum_fusion.6
  21.0 2.3 copy.41
  23.3 1.1 copy.42
  24.4 1.7 collective-permute-start.3
  26.2 1.6 pad_maximum_fusion.87
  28.3 1.1 copy.43
  29.4 2.0 copy.44
  31.4 2.3 pad_maximum_fusion
  35.0 8.3 %multiply_reduce_fusion.1 = (f32[322,130]{0,1:T(8,128)S(1)}, f32[322,130]{0,1:T(8,128)S(1)}, f32[4,322,130]{1,2,0:T(8,128)}, f32[4,322,130]{1,2,0:T(8,128)}) fusion(f32[4]{0:T(128)S(1)} %copy-done.27, f32[13,324,132]{1,2,0:T(8,128)S(1)} %pad_maximum_fusion, f32[322]{0:T(512)S(1)} %fusion.81, f32[13,320,2]{1,2,0:T(2,128)S(1)} %collective-permute-done.1, ...), kind=kLoop, calls=%fused_computation.40 | loop fusion | flops 10632440 | bytes 9592600 | tf_op jit(solution)/shard_map/reduce_sum | solution.py:145
  43.5 1.5 fusion.89
  45.0 4.7 %collective-permute-start.8 = (f32[320,1]{0,1:T(1,128)S(1)}, f32[320,1]{0,1:T(1,128)S(1)}, u32[]{:S(2)}, u32[]{:S(2)}) collective-permute-start(f32[320,1]{0,1:T(1,128)S(1)} %get-tuple-element.76), channel_id=1, source_target_pairs={{4,0},{8,4},{12,8},{16,12},{20,16},{24,20},{28,24},{0,28},{5,1},{9... | collective-permute-start | bytes 3848 | tf_op jit(solution)/shard_map/ppermute | solution.py:27
  49.8 1.3 collective-permute-done.8
  51.1 5.0 %collective-permute-done.9 = f32[320,1]{0,1:T(1,128)S(1)} collective-permute-done((f32[320,1]{0,1:T(1,128)S(1)}, f32[320,1]{0,1:T(1,128)S(1)}, u32[]{:S(2)}, u32[]{:S(2)}) %collective-permute-start.9) | collective-permute-done | bytes 1312 | tf_op jit(solution)/shard_map/ppermute | solution.py:25
  56.7 1.4 collective-permute-done.10
  58.1 2.6 collective-permute-done.11
  60.7 1.8 multiply_reduce_fusion.7
  62.5 37.3 %all-reduce.6 = (f32[]{:T(128)}, f32[]{:T(128)}) all-reduce(f32[]{:T(128)} %get-tuple-element.13, f32[]{:T(128)} %get-tuple-element.12), channel_id=1, replica_groups=mesh['gx'=8,'gy'=4] {'gx','gy'}, use_global_device_ids=true, to_apply=%region_3.4 | all-reduce | flops 2 | bytes 16 | tf_op jit(solution)/shard_map/psum | solution.py:73
  101.1 2.4 multiply_reduce_fusion.6
  103.5 41.9 %psum.58 = f32[]{:T(128)} all-reduce(f32[]{:T(128)} %get-tuple-element.25), channel_id=1, replica_groups=mesh['gx'=8,'gy'=4] {'gx','gy'}, use_global_device_ids=true, to_apply=%region_7.8 | all-reduce | flops 1 | bytes 8 | tf_op jit(solution)/shard_map/psum | solution.py:73
  146.8 1.0 multiply_add_fusion.4
  147.9 3.5 collective-permute-start.12
  151.4 1.3 collective-permute-done.12
  152.7 5.0 %collective-permute-done.13 = f32[320,1]{0,1:T(1,128)S(1)} collective-permute-done((f32[320,1]{0,1:T(1,128)S(1)}, f32[320,1]{0,1:T(1,128)S(1)}, u32[]{:S(2)}, u32[]{:S(2)}) %collective-permute-start.13) | collective-permute-done | bytes 1312 | tf_op jit(solution)/shard_map/ppermute | solution.py:25
  158.3 1.4 collective-permute-done.14
  159.7 2.3 collective-permute-done.15
  162.1 3.1 multiply_reduce_fusion.5
  165.1 37.1 %psum.59 = f32[]{:T(128)} all-reduce(f32[]{:T(128)} %get-tuple-element.23), channel_id=1, replica_groups=mesh['gx'=8,'gy'=4] {'gx','gy'}, use_global_device_ids=true, to_apply=%region_9.10 | all-reduce | flops 1 | bytes 8 | tf_op jit(solution)/shard_map/psum | solution.py:84
  203.6 2.5 multiply_reduce_fusion.4
  206.0 41.9 %psum.60 = f32[]{:T(128)} all-reduce(f32[]{:T(128)} %get-tuple-element.20), channel_id=1, replica_groups=mesh['gx'=8,'gy'=4] {'gx','gy'}, use_global_device_ids=true, to_apply=%region_11.12 | all-reduce | flops 1 | bytes 8 | tf_op jit(solution)/shard_map/psum | solution.py:73
  249.3 1.0 multiply_add_fusion.3
  250.4 3.6 collective-permute-start.16
  254.0 1.3 collective-permute-done.16
  255.3 5.0 %collective-permute-done.17 = f32[320,1]{0,1:T(1,128)S(1)} collective-permute-done((f32[320,1]{0,1:T(1,128)S(1)}, f32[320,1]{0,1:T(1,128)S(1)}, u32[]{:S(2)}, u32[]{:S(2)}) %collective-permute-start.17) | collective-permute-done | bytes 1312 | tf_op jit(solution)/shard_map/ppermute | solution.py:25
  260.9 1.4 collective-permute-done.18
  262.3 2.3 collective-permute-done.19
  264.7 3.0 multiply_reduce_fusion.3
  267.7 37.1 %psum.61 = f32[]{:T(128)} all-reduce(f32[]{:T(128)} %get-tuple-element.18), channel_id=1, replica_groups=mesh['gx'=8,'gy'=4] {'gx','gy'}, use_global_device_ids=true, to_apply=%region_13.14 | all-reduce | flops 1 | bytes 8 | tf_op jit(solution)/shard_map/psum | solution.py:84
  306.2 1.7 multiply_reduce_fusion.2
  307.8 41.9 %psum.62 = f32[]{:T(128)} all-reduce(f32[]{:T(128)} %multiply_reduce_fusion.2), channel_id=1, replica_groups=mesh['gx'=8,'gy'=4] {'gx','gy'}, use_global_device_ids=true, to_apply=%region_15.16 | all-reduce | flops 1 | bytes 8 | tf_op jit(solution)/shard_map/psum | solution.py:73
  351.1 1.2 multiply_add_fusion.2
  352.4 3.5 collective-permute-start.20
  355.9 1.3 collective-permute-done.20
  357.2 5.0 %collective-permute-done.21 = f32[320,1]{0,1:T(1,128)S(1)} collective-permute-done((f32[320,1]{0,1:T(1,128)S(1)}, f32[320,1]{0,1:T(1,128)S(1)}, u32[]{:S(2)}, u32[]{:S(2)}) %collective-permute-start.21) | collective-permute-done | bytes 1312 | tf_op jit(solution)/shard_map/ppermute | solution.py:25
  364.3 2.4 collective-permute-done.23
  366.7 1.8 fusion.93
  368.5 37.1 %psum.63 = f32[]{:T(128)} all-reduce(f32[]{:T(128)} %get-tuple-element.43), channel_id=1, replica_groups=mesh['gx'=8,'gy'=4] {'gx','gy'}, use_global_device_ids=true, to_apply=%region_17.18 | all-reduce | flops 1 | bytes 8 | tf_op jit(solution)/shard_map/psum | solution.py:84
  406.8 1.5 multiply_add_fusion.1
  408.4 4.1 collective-permute-start.24
  412.5 1.0 slice.428
  413.8 5.0 %collective-permute-done.25 = f32[320,1]{0,1:T(1,128)S(1)} collective-permute-done((f32[320,1]{0,1:T(1,128)S(1)}, f32[320,1]{0,1:T(1,128)S(1)}, u32[]{:S(2)}, u32[]{:S(2)}) %collective-permute-start.25) | collective-permute-done | bytes 1312 | tf_op jit(solution)/shard_map/ppermute | solution.py:25
  419.5 4.3 multiply_add_fusion
  424.6 2.2 copy.63
  426.8 1.0 fusion.28
  427.9 2.6 fusion.25
  430.5 2.2 copy.61
  432.7 1.1 copy.62
  (115 shorter events, 12.5 us)
Async XLA Ops:
  0.6 6.5 %copy-start.23 = (f32[4,320,128]{2,1,0:T(8,128)S(1)}, f32[4,320,128]{2,1,0:T(8,128)}, u32[]{:S(2)}) copy-start(f32[4,320,128]{2,1,0:T(8,128)} %param.10) | copy-start | bytes 1966084
  3.6 6.0 %copy-start.19 = (s32[320,128]{0,1:T(8,128)}, s32[320,128]{0,1:T(8,128)S(1)}, u32[]{:S(2)}) copy-start(s32[320,128]{0,1:T(8,128)S(1)} %copy.36) | copy-start | bytes 491524
  7.4 11.5 %copy-start.24 = (f32[320,128]{1,0:T(8,128)S(1)}, f32[320,128]{1,0:T(8,128)}, u32[]{:S(2)}) copy-start(f32[320,128]{1,0:T(8,128)} %param.14) | copy-start | bytes 491524
  9.6 6.2 %copy-start.16 = (f32[320,128]{0,1:T(8,128)}, f32[320,128]{0,1:T(8,128)S(1)}, u32[]{:S(2)}) copy-start(f32[320,128]{0,1:T(8,128)S(1)} %get-tuple-element.62) | copy-start | bytes 491524
  9.6 25.4 %copy-start.10 = (f32[1,320,128]{1,2,0:T(8,128)}, f32[1,320,128]{1,2,0:T(8,128)S(1)}, u32[]{:S(2)}) copy-start(f32[1,320,128]{1,2,0:T(8,128)S(1)} %get-tuple-element.63) | copy-start | bytes 491524
  9.6 10.2 %collective-permute-start = (f32[13,320,2]{1,2,0:T(2,128)S(1)}, f32[13,320,2]{1,2,0:T(2,128)S(1)}, u32[]{:S(2)}, u32[]{:S(2)}) collective-permute-start(f32[13,320,2]{1,2,0:T(2,128)S(1)} %get-tuple-element.38), channel_id=1, source_target_pairs={{0,4},{4,8},{8,12},{12,16},{16,20},{20,24},{24,28},{28,0},{1,5},{5... | collective-permute-start | bytes 99848 | tf_op jit(solution)/shard_map/ppermute | solution.py:25
  12.6 7.1 %collective-permute-start.1 = (f32[13,320,2]{1,2,0:T(2,128)S(1)}, f32[13,320,2]{1,2,0:T(2,128)S(1)}, u32[]{:S(2)}, u32[]{:S(2)}) collective-permute-start(f32[13,320,2]{1,2,0:T(2,128)S(1)} %get-tuple-element.39), channel_id=1, source_target_pairs={{4,0},{8,4},{12,8},{16,12},{20,16},{24,20},{28,24},{0,28},{5,1},{9... | collective-permute-start | bytes 99848 | tf_op jit(solution)/shard_map/ppermute | solution.py:27
  16.3 9.8 %collective-permute-start.4 = (f32[320,1]{0,1:T(1,128)}, f32[320,1]{0,1:T(1,128)}, u32[]{:S(2)}, u32[]{:S(2)}) collective-permute-start(f32[320,1]{0,1:T(1,128)} %get-tuple-element.78), channel_id=1, source_target_pairs={{4,0},{8,4},{12,8},{16,12},{20,16},{24,20},{28,24},{0,28},{5,1},{9... | collective-permute-start | bytes 3848 | tf_op jit(solution)/shard_map/ppermute | solution.py:27
  18.3 7.9 %collective-permute-start.5 = (f32[320,1]{0,1:T(1,128)}, f32[320,1]{0,1:T(1,128)}, u32[]{:S(2)}, u32[]{:S(2)}) collective-permute-start(f32[320,1]{0,1:T(1,128)} %get-tuple-element.77), channel_id=1, source_target_pairs={{0,4},{4,8},{8,12},{12,16},{16,20},{20,24},{24,28},{28,0},{1,5},{5... | collective-permute-start | bytes 3848 | tf_op jit(solution)/shard_map/ppermute | solution.py:25
  23.3 5.0 %collective-permute-start.2 = (f32[13,2,132]{2,1,0:T(2,128)}, f32[13,2,132]{2,1,0:T(2,128)}, u32[]{:S(2)}, u32[]{:S(2)}) collective-permute-start(f32[13,2,132]{2,1,0:T(2,128)} %copy.41), channel_id=1, source_target_pairs={{0,1},{1,2},{2,3},{3,0},{4,5},{5,6},{6,7},{7,4},{8,9},{9,10},{10,1... | collective-permute-start | bytes 41192 | tf_op jit(solution)/shard_map/ppermute | solution.py:25
  24.4 5.0 %collective-permute-start.3 = (f32[13,2,132]{2,1,0:T(2,128)}, f32[13,2,132]{2,1,0:T(2,128)}, u32[]{:S(2)}, u32[]{:S(2)}) collective-permute-start(f32[13,2,132]{2,1,0:T(2,128)} %copy.42), channel_id=1, source_target_pairs={{1,0},{2,1},{3,2},{0,3},{5,4},{6,5},{7,6},{4,7},{9,8},{10,9},{11,1... | collective-permute-start | bytes 41192 | tf_op jit(solution)/shard_map/ppermute | solution.py:27
  27.8 15.6 %collective-permute-start.6 = (f32[1,130]{0,1:T(8,128)}, f32[1,130]{0,1:T(8,128)}, u32[]{:S(2)}, u32[]{:S(2)}) collective-permute-start(f32[1,130]{0,1:T(8,128)} %get-tuple-element.58), channel_id=1, source_target_pairs={{1,0},{2,1},{3,2},{0,3},{5,4},{6,5},{7,6},{4,7},{9,8},{10,9},{11,1... | collective-permute-start | bytes 1568 | tf_op jit(solution)/shard_map/ppermute | solution.py:27
  27.8 15.6 %collective-permute-start.7 = (f32[1,130]{0,1:T(8,128)}, f32[1,130]{0,1:T(8,128)}, u32[]{:S(2)}, u32[]{:S(2)}) collective-permute-start(f32[1,130]{0,1:T(8,128)} %get-tuple-element.59), channel_id=1, source_target_pairs={{0,1},{1,2},{2,3},{3,0},{4,5},{5,6},{6,7},{7,4},{8,9},{9,10},{10,1... | collective-permute-start | bytes 1568 | tf_op jit(solution)/shard_map/ppermute | solution.py:25
  33.8 1.2 copy-start
  33.8 1.2 copy-start.27
  34.9 25.8 %copy-start.2 = (f32[322,130]{0,1:T(8,128)}, f32[322,130]{0,1:T(8,128)S(1)}, u32[]{:S(2)}) copy-start(f32[322,130]{0,1:T(8,128)S(1)} %get-tuple-element.47) | copy-start | bytes 502324
  34.9 25.8 %copy-start.4 = (f32[322,130]{0,1:T(8,128)}, f32[322,130]{0,1:T(8,128)S(1)}, u32[]{:S(2)}) copy-start(f32[322,130]{0,1:T(8,128)S(1)} %get-tuple-element.46) | copy-start | bytes 502324
  34.9 25.8 %copy-start.6 = (f32[322,130]{0,1:T(8,128)}, f32[322,130]{0,1:T(8,128)S(1)}, u32[]{:S(2)}) copy-start(f32[322,130]{0,1:T(8,128)S(1)} %get-tuple-element.48) | copy-start | bytes 502324
  34.9 25.8 %copy-start.8 = (f32[322,130]{0,1:T(8,128)}, f32[322,130]{0,1:T(8,128)S(1)}, u32[]{:S(2)}) copy-start(f32[322,130]{0,1:T(8,128)S(1)} %get-tuple-element.49) | copy-start | bytes 502324
  34.9 8.5 %copy-start.17 = (f32[320,128]{0,1:T(8,128)S(1)}, f32[320,128]{0,1:T(8,128)}, u32[]{:S(2)}) copy-start(f32[320,128]{0,1:T(8,128)} %copy-done.16) | copy-start | bytes 491524
  35.0 8.5 %copy-start.20 = (s32[320,128]{0,1:T(8,128)S(1)}, s32[320,128]{0,1:T(8,128)}, u32[]{:S(2)}) copy-start(s32[320,128]{0,1:T(8,128)} %copy-done.19) | copy-start | bytes 491524
  35.0 8.5 %copy-start.22 = (f32[320,128]{0,1:T(8,128)S(1)}, f32[320,128]{0,1:T(8,128)}, u32[]{:S(2)}) copy-start(f32[320,128]{0,1:T(8,128)} %copy.48) | copy-start | bytes 491524
  45.0 17.5 %copy-start.13 = (f32[320,128]{0,1:T(8,128)}, f32[320,128]{0,1:T(8,128)S(1)}, u32[]{:S(2)}) copy-start(f32[320,128]{0,1:T(8,128)S(1)} %get-tuple-element.29) | copy-start | bytes 491524
  45.0 17.5 %copy-start.21 = (f32[320,128]{0,1:T(8,128)}, f32[320,128]{0,1:T(8,128)S(1)}, u32[]{:S(2)}) copy-start(f32[320,128]{0,1:T(8,128)S(1)} %get-tuple-element.30) | copy-start | bytes 491524
  45.0 6.0 %collective-permute-start.8 = (f32[320,1]{0,1:T(1,128)S(1)}, f32[320,1]{0,1:T(1,128)S(1)}, u32[]{:S(2)}, u32[]{:S(2)}) collective-permute-start(f32[320,1]{0,1:T(1,128)S(1)} %get-tuple-element.76), channel_id=1, source_target_pairs={{4,0},{8,4},{12,8},{16,12},{20,16},{24,20},{28,24},{0,28},{5,1},{9... | collective-permute-start | bytes 3848 | tf_op jit(solution)/shard_map/ppermute | solution.py:27
  49.8 6.3 %collective-permute-start.9 = (f32[320,1]{0,1:T(1,128)S(1)}, f32[320,1]{0,1:T(1,128)S(1)}, u32[]{:S(2)}, u32[]{:S(2)}) collective-permute-start(f32[320,1]{0,1:T(1,128)S(1)} %get-tuple-element.75), channel_id=1, source_target_pairs={{0,4},{4,8},{8,12},{12,16},{16,20},{20,24},{24,28},{28,0},{1,5},{5... | collective-permute-start | bytes 3848 | tf_op jit(solution)/shard_map/ppermute | solution.py:25
  56.1 2.0 collective-permute-start.10
  56.2 4.5 %collective-permute-start.11 = (f32[1,130]{0,1:T(8,128)S(1)}, f32[1,130]{0,1:T(8,128)S(1)}, u32[]{:S(2)}, u32[]{:S(2)}) collective-permute-start(f32[1,130]{0,1:T(8,128)S(1)} %get-tuple-element.57), channel_id=1, source_target_pairs={{0,1},{1,2},{2,3},{3,0},{4,5},{5,6},{6,7},{7,4},{8,9},{9,10},{10,1... | collective-permute-start | bytes 1568 | tf_op jit(solution)/shard_map/ppermute | solution.py:25
  147.8 14.2 %copy-start.11 = (f32[320,128]{0,1:T(8,128)}, f32[320,128]{0,1:T(8,128)S(1)}, u32[]{:S(2)}) copy-start(f32[320,128]{0,1:T(8,128)S(1)} %multiply_add_fusion.4) | copy-start | bytes 491524
  147.9 4.8 %collective-permute-start.12 = (f32[320,1]{0,1:T(1,128)S(1)}, f32[320,1]{0,1:T(1,128)S(1)}, u32[]{:S(2)}, u32[]{:S(2)}) collective-permute-start(f32[320,1]{0,1:T(1,128)S(1)} %get-tuple-element.74), channel_id=1, source_target_pairs={{4,0},{8,4},{12,8},{16,12},{20,16},{24,20},{28,24},{0,28},{5,1},{9... | collective-permute-start | bytes 3848 | tf_op jit(solution)/shard_map/ppermute | solution.py:27
  151.4 6.3 %collective-permute-start.13 = (f32[320,1]{0,1:T(1,128)S(1)}, f32[320,1]{0,1:T(1,128)S(1)}, u32[]{:S(2)}, u32[]{:S(2)}) collective-permute-start(f32[320,1]{0,1:T(1,128)S(1)} %get-tuple-element.73), channel_id=1, source_target_pairs={{0,4},{4,8},{8,12},{12,16},{16,20},{20,24},{24,28},{28,0},{1,5},{5... | collective-permute-start | bytes 3848 | tf_op jit(solution)/shard_map/ppermute | solution.py:25
  157.7 2.0 collective-permute-start.14
  157.8 4.3 collective-permute-start.15
  250.4 14.3 %copy-start.12 = (f32[320,128]{0,1:T(8,128)}, f32[320,128]{0,1:T(8,128)S(1)}, u32[]{:S(2)}) copy-start(f32[320,128]{0,1:T(8,128)S(1)} %multiply_add_fusion.3) | copy-start | bytes 491524
  250.4 4.9 %collective-permute-start.16 = (f32[320,1]{0,1:T(1,128)S(1)}, f32[320,1]{0,1:T(1,128)S(1)}, u32[]{:S(2)}, u32[]{:S(2)}) collective-permute-start(f32[320,1]{0,1:T(1,128)S(1)} %get-tuple-element.72), channel_id=1, source_target_pairs={{4,0},{8,4},{12,8},{16,12},{20,16},{24,20},{28,24},{0,28},{5,1},{9... | collective-permute-start | bytes 3848 | tf_op jit(solution)/shard_map/ppermute | solution.py:27
  254.0 6.3 %collective-permute-start.17 = (f32[320,1]{0,1:T(1,128)S(1)}, f32[320,1]{0,1:T(1,128)S(1)}, u32[]{:S(2)}, u32[]{:S(2)}) collective-permute-start(f32[320,1]{0,1:T(1,128)S(1)} %get-tuple-element.71), channel_id=1, source_target_pairs={{0,4},{4,8},{8,12},{12,16},{16,20},{20,24},{24,28},{28,0},{1,5},{5... | collective-permute-start | bytes 3848 | tf_op jit(solution)/shard_map/ppermute | solution.py:25
  260.3 2.0 collective-permute-start.18
  260.4 4.3 collective-permute-start.19
  351.1 15.6 %copy-start.3 = (f32[322,130]{0,1:T(8,128)S(1)}, f32[322,130]{0,1:T(8,128)}, u32[]{:S(2)}) copy-start(f32[322,130]{0,1:T(8,128)} %copy-done.2) | copy-start | bytes 502324
  351.1 15.6 %copy-start.5 = (f32[322,130]{0,1:T(8,128)S(1)}, f32[322,130]{0,1:T(8,128)}, u32[]{:S(2)}) copy-start(f32[322,130]{0,1:T(8,128)} %copy-done.4) | copy-start | bytes 502324
  351.1 15.6 %copy-start.7 = (f32[322,130]{0,1:T(8,128)S(1)}, f32[322,130]{0,1:T(8,128)}, u32[]{:S(2)}) copy-start(f32[322,130]{0,1:T(8,128)} %copy-done.6) | copy-start | bytes 502324
  351.1 15.6 %copy-start.9 = (f32[322,130]{0,1:T(8,128)S(1)}, f32[322,130]{0,1:T(8,128)}, u32[]{:S(2)}) copy-start(f32[322,130]{0,1:T(8,128)} %copy-done.8) | copy-start | bytes 502324
  352.4 4.8 %collective-permute-start.20 = (f32[320,1]{0,1:T(1,128)S(1)}, f32[320,1]{0,1:T(1,128)S(1)}, u32[]{:S(2)}, u32[]{:S(2)}) collective-permute-start(f32[320,1]{0,1:T(1,128)S(1)} %get-tuple-element.70), channel_id=1, source_target_pairs={{4,0},{8,4},{12,8},{16,12},{20,16},{24,20},{28,24},{0,28},{5,1},{9... | collective-permute-start | bytes 3848 | tf_op jit(solution)/shard_map/ppermute | solution.py:27
  355.9 6.3 %collective-permute-start.21 = (f32[320,1]{0,1:T(1,128)S(1)}, f32[320,1]{0,1:T(1,128)S(1)}, u32[]{:S(2)}, u32[]{:S(2)}) collective-permute-start(f32[320,1]{0,1:T(1,128)S(1)} %get-tuple-element.69), channel_id=1, source_target_pairs={{0,4},{4,8},{8,12},{12,16},{16,20},{20,24},{24,28},{28,0},{1,5},{5... | collective-permute-start | bytes 3848 | tf_op jit(solution)/shard_map/ppermute | solution.py:25
  362.3 2.0 collective-permute-start.22
  362.3 4.4 %collective-permute-start.23 = (f32[1,130]{0,1:T(8,128)S(1)}, f32[1,130]{0,1:T(8,128)S(1)}, u32[]{:S(2)}, u32[]{:S(2)}) collective-permute-start(f32[1,130]{0,1:T(8,128)S(1)} %get-tuple-element.51), channel_id=1, source_target_pairs={{0,1},{1,2},{2,3},{3,0},{4,5},{5,6},{6,7},{7,4},{8,9},{9,10},{10,1... | collective-permute-start | bytes 1568 | tf_op jit(solution)/shard_map/ppermute | solution.py:25
  406.8 12.6 %copy-start.1 = (f32[13,2,132]{1,2,0:T(8,128)S(1)}, f32[13,2,132]{1,2,0:T(8,128)}, u32[]{:S(2)}) copy-start(f32[13,2,132]{1,2,0:T(8,128)} %copy.44) | copy-start | bytes 41188
  408.3 10.4 %copy-start.14 = (f32[320,128]{0,1:T(8,128)}, f32[320,128]{0,1:T(8,128)S(1)}, u32[]{:S(2)}) copy-start(f32[320,128]{0,1:T(8,128)S(1)} %multiply_add_fusion.1) | copy-start | bytes 491524
  408.4 5.4 %collective-permute-start.24 = (f32[320,1]{0,1:T(1,128)S(1)}, f32[320,1]{0,1:T(1,128)S(1)}, u32[]{:S(2)}, u32[]{:S(2)}) collective-permute-start(f32[320,1]{0,1:T(1,128)S(1)} %get-tuple-element.67), channel_id=1, source_target_pairs={{4,0},{8,4},{12,8},{16,12},{20,16},{24,20},{28,24},{0,28},{5,1},{9... | collective-permute-start | bytes 3848 | tf_op jit(solution)/shard_map/ppermute | solution.py:27
  412.5 6.3 %collective-permute-start.25 = (f32[320,1]{0,1:T(1,128)S(1)}, f32[320,1]{0,1:T(1,128)S(1)}, u32[]{:S(2)}, u32[]{:S(2)}) collective-permute-start(f32[320,1]{0,1:T(1,128)S(1)} %get-tuple-element.66), channel_id=1, source_target_pairs={{0,4},{4,8},{8,12},{12,16},{16,20},{20,24},{24,28},{28,0},{1,5},{5... | collective-permute-start | bytes 3848 | tf_op jit(solution)/shard_map/ppermute | solution.py:25
  418.8 0.7 copy-start.25
  419.4 7.4 %collective-permute-start.26 = (f32[1,130]{0,1:T(8,128)}, f32[1,130]{0,1:T(8,128)}, u32[]{:S(2)}, u32[]{:S(2)}) collective-permute-start(f32[1,130]{0,1:T(8,128)} %pad_maximum_fusion.71), channel_id=1, source_target_pairs={{1,0},{2,1},{3,2},{0,3},{5,4},{6,5},{7,6},{4,7},{9,8},{10,9},{11,1... | collective-permute-start | bytes 1568 | tf_op jit(solution)/shard_map/ppermute | solution.py:27
  419.4 4.3 %copy-start.15 = (f32[320,128]{0,1:T(8,128)S(1)}, f32[320,128]{0,1:T(8,128)}, u32[]{:S(2)}) copy-start(f32[320,128]{0,1:T(8,128)} %copy-done.14) | copy-start | bytes 491524
  419.5 7.4 %copy-start.26 = (f32[320,1]{0,1:T(1,128)S(1)}, f32[320,1]{0,1:T(1,128)}, u32[]{:S(2)}) copy-start(f32[320,1]{0,1:T(1,128)} %copy-done.25) | copy-start | bytes 3844
  423.8 4.1 copy-start.18
where the time goes:
time: 436 us; the launch traced here: 434 us
  blocking collectives  274 us (63%)
  other arithmetic  50.1 us (11%)
  waiting for transfers between devices  44.9 us (10%)
  starting transfers between devices  32.1 us (7%)
  local copies, waits for them, and re-layouts  22 us (5%)
  between operations  10.5 us (2%)
    psum x4, blocking collectives, norm_total(): return lax.psum(jnp.sum(residual * precond), ('gx', 'gy'))  163 us
    psum x3, blocking collectives, conjugate(): alpha = rz_now / lax.psum(jnp.sum(direction * image), ('gx', 'gy'))  111 us
    ppermute x13, waiting for transfers between devices, padded_2(): lax.ppermute(tail, axis, [(i, (i + 1) % count) for i in range(count)])  34.6 us
    ppermute x14, starting transfers between devices, padded_2(): lax.ppermute(head, axis, [((i + 1) % count, i) for i in range(count)])  26.5 us
    unnamed x67, local copies, waits for them, and re-layouts  13.5 us
    ppermute x14, waiting for transfers between devices, padded_2(): lax.ppermute(head, axis, [((i + 1) % count, i) for i in range(count)])  10.4 us
  transfers between devices with their start and end apart: 27, of which 18 were waited for; matrix products, arithmetic and copies ran while one was open for 7% of the time, Pallas kernels for 0%

commit v1 on v0

v1 whole, which is shorter than its diff:
```python
import jax
import jax.numpy as jnp
from jax import lax
from jax.experimental import pallas as pl
from jax.experimental.pallas import tpu as pltpu
from jax.sharding import PartitionSpec as P

BX = 128
BY = 40
ITERS = 4

step_time = 0.2
viscosity = 0.5
diffusivity = 0.5
vertical = 0.5
gravity = 1.0

SUB = 8
LANES = 128
HALF = LANES // 2
PLANES = ("U", "G", "V", "H", "wet", "start", "helm")
WIDTHS = (ITERS + 2, ITERS + 1, ITERS + 1, ITERS, ITERS + 2, ITERS + 1, ITERS)
OFFSETS = tuple(sum(WIDTHS[:i]) for i in range(len(WIDTHS)))
EDGE = sum(WIDTHS)
NP = len(PLANES)
f32 = jnp.float32


def roll(x, shift, axis=1):
    shift = shift % x.shape[axis]
    return x if shift == 0 else pltpu.roll(x, shift, axis)


def lane_of(x):
    return lax.broadcasted_iota(jnp.int32, x.shape, 1)


def thickness(levels):
    return [(2 * k + 1) / (levels * levels) for k in range(levels)]


def mixed_weights(levels):
    thick = thickness(levels)
    out = list(thick)
    for k in range(levels - 1):
        move = step_time * vertical * (thick[k] - thick[k + 1])
        out[k + 1] += move
        out[k] -= move
    return out


def weighted(weights, fields):
    total = weights[0] * fields[0]
    for w, f in zip(weights[1:], fields[1:]):
        total = total + w * f
    return total


def planes_of(us, vs, pressure_old, depth, helm, land, domain, first_row, total_rows):
    levels = len(us)
    thick, mixed = thickness(levels), mixed_weights(levels)
    row = first_row + lax.broadcasted_iota(jnp.int32, us[0].shape, 0)
    coriolis = 0.2 + 0.6 * ((row.astype(f32) + 0.5) / total_rows)
    u_sum, v_sum = weighted(thick, us), weighted(thick, vs)
    east = weighted(mixed, us) + step_time * coriolis * v_sum
    north = weighted(mixed, vs) - step_time * coriolis * u_sum
    mask = land.astype(f32) * domain
    return (u_sum, east, v_sum, north, depth * mask, mask * pressure_old, helm)


def place():
    return lax.axis_index("gx"), lax.axis_index("gy")


def domain_at(tropic_ref, row_dev, col_dev, rows, row):
    block = row_dev * (rows // BY) + row // BY
    return jnp.where(tropic_ref[block, col_dev] >= 0, 1.0, 0.0).astype(f32)


def rim_kernel(
    rows, total_rows, u, v, t, p, depth, helm, land, tropic, low_out, high_out, s3, s2, si, sems
):
    col_dev, row_dev = place()
    levels = u.shape[0]
    copies = []
    for side, r0 in enumerate((0, rows - SUB)):
        for i, ref in enumerate((u, v, t)):
            copies.append((ref.at[:, pl.ds(r0, SUB), :], s3.at[side, i]))
        for i, ref in enumerate((p, depth, helm)):
            copies.append((ref.at[pl.ds(r0, SUB), :], s2.at[side, i]))
        copies.append((land.at[pl.ds(r0, SUB), :], si.at[side]))
    copies = [pltpu.make_async_copy(a, b, sems.at[i]) for i, (a, b) in enumerate(copies)]
    for c in copies:
        c.start()
    for c in copies:
        c.wait()
    for side, (r0, out) in enumerate(((0, low_out), (rows - SUB, high_out))):
        domain = domain_at(tropic, row_dev, col_dev, rows, r0)
        us = [s3[side, 0, k] for k in range(levels)]
        vs = [s3[side, 1, k] for k in range(levels)]
        planes = planes_of(
            us, vs, s2[side, 0], s2[side, 1], s2[side, 2], si[side], domain,
            row_dev * rows + r0, total_rows,
        )
        for i, plane in enumerate(planes):
            out[pl.ds(SUB * i, SUB), :] = plane
        edge = 0 if side == 0 else SUB - 1
        for i in range(3):
            for k in range(levels):
                n = SUB * NP + i * levels + k
                out[n : n + 1, :] = s3[side, i, k, edge : edge + 1, :]
        used = SUB * NP + 3 * levels
        if used < out.shape[0]:
            out[used:, :] = jnp.zeros((out.shape[0] - used, LANES), f32)


def pack_pair(low_fields, high_fields, extra_low, extra_high, to_west):
    shape = low_fields[0].shape
    lane = lax.broadcasted_iota(jnp.int32, shape, 1)
    out = jnp.zeros(shape, f32)
    for base, fields, extra in ((0, low_fields, extra_low), (HALF, high_fields, extra_high)):
        for f, w, off in zip(fields, WIDTHS, OFFSETS):
            lo = base + off
            first = 0 if to_west else LANES - w
            out = jnp.where((lane >= lo) & (lane < lo + w), roll(f, lo - first), out)
        for i, f in enumerate(extra):
            lo = base + EDGE + i
            first = 0 if to_west else LANES - 1
            out = jnp.where(lane == lo, roll(f, lo - first), out)
    return out


def plane_kernel(rows, total_rows, u, v, t, p, depth, helm, land, tropic, planes, west, east):
    col_dev, row_dev = place()
    levels = u.shape[0]
    half = rows // 2

    def at(r):
        r = pl.multiple_of(r, SUB)
        here = pl.ds(r, SUB)
        us = [u[k, here, :] for k in range(levels)]
        vs = [v[k, here, :] for k in range(levels)]
        ts = [t[k, here, :] for k in range(levels)]
        domain = domain_at(tropic, row_dev, col_dev, rows, r)
        out = planes_of(
            us, vs, p[here, :], depth[here, :], helm[here, :], land[here, :], domain,
            row_dev * rows + r, total_rows,
        )
        for i, plane in enumerate(out):
            planes[i, here, :] = plane
        return out, us + vs + ts

    unroll = 4

    def body(i, carry):
        for j in range(unroll):
            r = (i * unroll + j) * SUB
            low, extra_low = at(r)
            high, extra_high = at(r + half)
            here = pl.ds(pl.multiple_of(r, SUB), SUB)
            west[here, :] = pack_pair(low, high, extra_low, extra_high, True)
            east[here, :] = pack_pair(low, high, extra_low, extra_high, False)
        return carry

    lax.fori_loop(0, half // (SUB * unroll), body, 0)


def corner_kernel(from_low, from_high, west_in, east_in, west, east):
    low = [from_low[pl.ds(SUB * i, SUB), :] for i in range(NP)]
    high = [from_high[pl.ds(SUB * i, SUB), :] for i in range(NP)]
    west[...] = pack_pair(low, high, [], [], True)
    east[...] = pack_pair(low, high, [], [], False)


def shifted(c, h):
    lane = lane_of(c)
    rc, rh = roll(c, -1), roll(h, -1)
    last = lane == LANES - 1
    east = jnp.where(last, rh, rc), jnp.where(last, rc, rh)
    rc, rh = roll(c, 1), roll(h, 1)
    first = lane == 0
    west = jnp.where(first, rh, rc), jnp.where(first, rc, rh)
    return east, west


CH = 24


def solve_kernel(
    rows, planes, from_low, from_high, from_west, from_east,
    basis, faces, partial, F, face_e, face_n, flow_e, flow_n, T, coef, diag,
):
    ext = rows + 2 * SUB
    half = rows // 2
    top = ext + SUB
    zero8 = jnp.zeros((SUB, LANES), f32)
    for c in range(2):
        for r in (0, top):
            for i in range(NP):
                F[i, c, pl.ds(r, SUB), :] = zero8
            face_e[c, pl.ds(r, SUB), :] = zero8
            face_n[c, pl.ds(r, SUB), :] = zero8
            flow_n[c, pl.ds(r, SUB), :] = zero8
            for k in range(ITERS):
                T[k, c, pl.ds(r, SUB), :] = zero8

    def unpack(dst, src, base):
        e, w = from_east[src, :], from_west[src, :]
        lane = lane_of(e)
        for i in range(NP):
            lo = base + OFFSETS[i]
            width = WIDTHS[i]
            he = roll(e, -lo)
            hw = roll(w, LANES - width - lo)
            h = jnp.where(lane < width, he, jnp.where(lane >= LANES - width, hw, 0.0))
            F[i, 1, dst, :] = h

    for i in range(NP):
        F[i, 0, pl.ds(SUB, SUB), :] = from_low[pl.ds(SUB * i, SUB), :]
        F[i, 0, pl.ds(SUB + SUB + rows, SUB), :] = from_high[pl.ds(SUB * i, SUB), :]
        F[i, 0, pl.ds(2 * SUB, rows), :] = planes[i]
    unpack(pl.ds(SUB, SUB), pl.ds(half, SUB), 0)
    unpack(pl.ds(2 * SUB + rows, SUB), pl.ds(half, SUB), HALF)
    step = 40
    for r in range(0, half, step):
        unpack(pl.ds(2 * SUB + r, step), pl.ds(r, step), 0)
        unpack(pl.ds(2 * SUB + half + r, step), pl.ds(r, step), HALF)

    iU, iG, iV, iH, iW, iS, iM = range(NP)
    chunks = [(SUB + r) for r in range(0, ext, CH)]
    assert ext % CH == 0
    both = (0, 1)

    def load(ref, idx, r, d=0):
        return tuple(ref[idx + (c, slice(r + d, r + d + CH), slice(None))] for c in both)

    def store(ref, idx, r, value):
        for c in both:
            ref[idx + (c, slice(r, r + CH), slice(None))] = value[c]

    def around(ref, idx, r):
        x = load(ref, idx, r)
        e, w = shifted(*x)
        return x, e, w, load(ref, idx, r, 1), load(ref, idx, r, -1)

    def stage_faces(r):
        x, e, _, n, _ = around(F, (iW,), r)
        store(face_e, (), r, tuple(jnp.minimum(x[c], e[c]) for c in both))
        store(face_n, (), r, tuple(jnp.minimum(x[c], n[c]) for c in both))

    def stage_flows(r):
        fe, fn, fs = load(face_e, (), r), load(face_n, (), r), load(face_n, (), r, -1)
        _, fw = shifted(*fe)
        wet = load(F, (iW,), r)
        for field, base, out in ((iU, iG, flow_e), (iV, iH, flow_n)):
            x, e, w, n, s = around(F, (field,), r)
            g = load(F, (base,), r)
            flow = []
            for c in both:
                d = (
                    fe[c] * (e[c] - x[c]) + fw[c] * (w[c] - x[c])
                    + fn[c] * (n[c] - x[c]) + fs[c] * (s[c] - x[c])
                )
                flow.append(wet[c] * (g[c] + (step_time * viscosity) * d))
            store(out, (), r, flow)

    def core_rows(r):
        lo, hi = max(r, 2 * SUB), min(r + CH, 2 * SUB + rows)
        return lo - r, hi - r

    sums = [None] * (2 * ITERS)

    def add_sum(i, r, value):
        lo, hi = core_rows(r)
        for q in range(lo, hi, SUB):
            part = value[q : q + SUB]
            sums[i] = part if sums[i] is None else sums[i] + part

    def stage_residual(r):
        fe, fn, fs = load(face_e, (), r), load(face_n, (), r), load(face_n, (), r, -1)
        _, fw = shifted(*fe)
        wet, helm = load(F, (iW,), r), load(F, (iM,), r)
        ef = load(flow_e, (), r)
        _, efw = shifted(*ef)
        nf, nfs = load(flow_n, (), r), load(flow_n, (), r, -1)
        x, e, w, n, s = around(F, (iS,), r)
        lo, hi = core_rows(r)
        for c in both:
            mask = wet[c] > 0.0
            force = jnp.where(mask, -(ef[c] - efw[c]) - (nf[c] - nfs[c]), 0.0)
            d = helm[c] + fe[c] + fw[c] + fn[c] + fs[c]
            res = force - (
                d * x[c] - fe[c] * e[c] - fw[c] * w[c] - fn[c] * n[c] - fs[c] * s[c]
            )
            inv = 1.0 / jnp.where(d > 0.0, d, 1.0)
            z = res * inv
            here = slice(r, r + CH)
            T[0, c, here, :] = z
            for i, f in enumerate((fe, fw, fn, fs)):
                coef[i, c, here, :] = f[c] * inv
            if c == 0:
                diag[here, :] = d
                add_sum(0, r, res * z)
                for i, f in enumerate((fe, fw, fn, fs)):
                    faces[i, r + lo - 2 * SUB : r + hi - 2 * SUB, :] = f[0][lo:hi]

    def stage_step(k, r):
        x, e, w, n, s = around(T, (k,), r)
        here = slice(r, r + CH)
        for c in both if k + 1 < ITERS else (0,):
            y = (
                coef[0, c, here, :] * e[c] + coef[1, c, here, :] * w[c]
                + coef[2, c, here, :] * n[c] + coef[3, c, here, :] * s[c]
            )
            if k > 0:
                y = 2.0 * y - T[k - 1, c, here, :]
            if k + 1 < ITERS:
                T[k + 1, c, here, :] = y
            if c == 0:
                d = diag[here, :]
                add_sum(2 * k + 1, r, d * x[c] * y)
                if k + 1 < ITERS:
                    add_sum(2 * k + 2, r, d * y * y)

    stages = [stage_faces, stage_flows, stage_residual]
    stages += [lambda r, k=k: stage_step(k, r) for k in range(ITERS)]
    lags = [0]
    for _ in stages[1:]:
        lags.append(lags[-1] + 1)
    lags = [0, 1, 2] + [2 + 2 * (k + 1) for k in range(ITERS)]
    for i in range(len(chunks) + lags[-1]):
        for stage, lag in zip(stages, lags):
            if 0 <= i - lag < len(chunks):
                stage(chunks[i - lag])

    for c in both:
        basis[0, c] = F[iS, c, SUB : SUB + ext, :]
        for k in range(ITERS):
            basis[k + 1, c] = T[k, c, SUB : SUB + ext, :]
    lane = lax.broadcasted_iota(jnp.int32, (1, LANES), 1)
    line = jnp.zeros((1, LANES), f32)
    for i, total in enumerate(sums):
        one = jnp.sum(jnp.sum(total, axis=0, keepdims=True), axis=1, keepdims=True)
        line = jnp.where(lane == i, one, line)
    partial[...] = jnp.broadcast_to(line, partial.shape)


def coefficients(m):
    n = ITERS

    def gram(i, j):
        return 0.5 * (m[i + j] + m[abs(i - j)])

    G = [[gram(i, j) for j in range(n)] for i in range(n)]
    H = [[gram(i, j) - 0.5 * (gram(i, j + 1) + gram(i, abs(j - 1))) for j in range(n)] for i in range(n)]
    zero = jnp.zeros_like(m[0])

    def quad(a, Q):
        total = zero
        for i in range(len(a)):
            total = total + a[i] * a[i] * Q[i][i]
            for j in range(i):
                total = total + 2.0 * a[i] * a[j] * Q[i][j]
        return total

    def ratio(a, b):
        return jnp.where(b > 0.0, a / jnp.where(b > 0.0, b, 1.0), 0.0)

    z = [jnp.ones_like(zero)]
    p = list(z)
    x = [zero] * n
    rz = m[0]
    for it in range(n):
        alpha = ratio(rz, quad(p, H))
        for i in range(len(p)):
            x[i] = x[i] + alpha * p[i]
        if it + 1 == n:
            break
        image = p + [zero]
        for j in range(len(p)):
            if j == 0:
                image[1] = image[1] - p[0]
            else:
                image[j + 1] = image[j + 1] - 0.5 * p[j]
                image[j - 1] = image[j - 1] - 0.5 * p[j]
        z = [a - alpha * b for a, b in zip(z + [zero], image)]
        rz_next = quad(z, G)
        beta = ratio(rz_next, rz)
        p = [a + beta * b for a, b in zip(z, p + [zero])]
        rz = rz_next
    return x


def finish_kernel(
    rows, total_rows, u, v, t, land, clinic, parts, basis, faces, from_low, from_high, from_west,
    from_east, u_out, v_out, t_out, p_out, pres,
):
    col_dev, row_dev = place()
    levels = u.shape[0]
    half = rows // 2
    lane1 = lax.broadcasted_iota(jnp.int32, (1, LANES), 1)
    line = jnp.sum(parts[...], axis=0, keepdims=True)
    sums = []
    for i in range(2 * ITERS):
        one = jnp.sum(jnp.where(lane1 == i, line, 0.0), axis=1, keepdims=True)
        sums.append(jnp.broadcast_to(one, (1, LANES)))
    m = sums[:2] + [2.0 * s - sums[i % 2] for i, s in enumerate(sums[2:])]
    x = coefficients(m)
    ext = rows + 2 * SUB
    for r in range(0, ext, CH):
        here = slice(r, r + CH)
        for c in range(2):
            total = basis[0, c, here, :]
            for k in range(ITERS):
                total = total + x[k] * basis[k + 1, c, here, :]
            pres[c, here, :] = total

    for r in range(0, rows, BY):
        block = row_dev * (rows // BY) + r // BY
        active = clinic[block, col_dev].astype(f32)
        here = pl.ds(r, BY)
        keep = land[here, :].astype(f32) * active
        rest = 1.0 - active
        pc = pres[0, SUB + r : SUB + r + BY, :]
        ph = pres[1, SUB + r : SUB + r + BY, :]
        p_out[here, :] = pc
        lane = lane_of(pc)
        first, last = lane == 0, lane == LANES - 1
        grad_x = jnp.where(last, roll(ph, -1), roll(pc, -1)) - pc
        grad_y = pres[0, SUB + r + 1 : SUB + r + BY + 1, :] - pc
        fe, fw, fn, fs = (faces[i, here, :] for i in range(4))
        row = row_dev * rows + r + lax.broadcasted_iota(jnp.int32, (BY, LANES), 0)
        coriolis = 0.2 + 0.6 * ((row.astype(f32) + 0.5) / total_rows)
        src = pl.ds(r % half, BY)
        base = HALF * (r // half) + EDGE

        def around(ref, which, k):
            n_row = SUB * NP + which * levels + k
            a = ref[k, here, :]
            lo = base + which * levels + k
            e = jnp.where(last, roll(from_east[src, :], LANES - 1 - lo), roll(a, -1))
            w = jnp.where(first, roll(from_west[src, :], -lo), roll(a, 1))
            if r + BY < rows:
                n = ref[k, r + 1 : r + BY + 1, :]
            else:
                n = jnp.concatenate([a[1:], from_high[n_row : n_row + 1, :]], 0)
            if r > 0:
                s = ref[k, r - 1 : r + BY - 1, :]
            else:
                s = jnp.concatenate([from_low[n_row : n_row + 1, :], a[:-1]], 0)
            return a, e, w, n, s

        def diffuse(a, e, w, n, s):
            return fe * (e - a) + fw * (w - a) + fn * (n - a) + fs * (s - a)

        def mixing(ref, k, a):
            total = None
            if k + 1 < levels:
                total = ref[k + 1, here, :] - a
            if k > 0:
                down = a - ref[k - 1, here, :]
                total = -down if total is None else total - down
            return jnp.zeros_like(a) if total is None else total

        for k in range(levels):
            ua = around(u, 0, k)
            va = around(v, 1, k)
            ta = around(t, 2, k)
            uc, vc, tc = ua[0], va[0], ta[0]
            u_star = uc + step_time * (
                vertical * mixing(u, k, uc) + viscosity * diffuse(*ua) + coriolis * vc
            )
            v_star = vc + step_time * (
                vertical * mixing(v, k, vc) + viscosity * diffuse(*va) - coriolis * uc
            )
            raw = tc + step_time * (
                vertical * mixing(t, k, tc) + diffusivity * diffuse(*ta)
                - 0.5 * (uc * (ta[1] - ta[2]) + vc * (ta[3] - ta[4]))
            )
            u_out[k, here, :] = keep * (u_star - gravity * grad_x) + rest * uc
            v_out[k, here, :] = keep * (v_star - gravity * grad_y) + rest * vc
            t_out[k, here, :] = keep * raw + rest * tc


VMEM = pl.BlockSpec(memory_space=pltpu.VMEM)
SMEM = pl.BlockSpec(memory_space=pltpu.SMEM)
ANY = pl.BlockSpec(memory_space=pl.ANY)


def shape(*dims):
    return jax.ShapeDtypeStruct(dims, f32)


def on_device(
    velocity_u, velocity_v, tracer, pressure_old, depth, helm, land_mask, clinic_map, tropic_map
):
    levels, rows, cols = velocity_u.shape
    nx, ny = lax.axis_size("gx"), lax.axis_size("gy")
    total_rows = rows * ny
    assert cols == LANES == BX and rows % BY == 0 and rows % (2 * BY) == 0
    assert EDGE + 3 * levels <= HALF and ITERS + 2 <= SUB
    half = rows // 2
    ext = rows + 2 * SUB
    strip = -(-(SUB * NP + 3 * levels) // SUB) * SUB
    fields = (velocity_u, velocity_v, tracer, pressure_old, depth, helm, land_mask, tropic_map)

    def params(**kw):
        return pltpu.CompilerParams(vmem_limit_bytes=40 << 20, **kw)

    low, high = pl.pallas_call(
        lambda *a: rim_kernel(rows, total_rows, *a),
        out_shape=(shape(strip, LANES), shape(strip, LANES)),
        in_specs=[ANY] * 7 + [SMEM],
        out_specs=(VMEM, VMEM),
        scratch_shapes=[
            pltpu.VMEM((2, 3, levels, SUB, LANES), f32),
            pltpu.VMEM((2, 3, SUB, LANES), f32),
            pltpu.VMEM((2, SUB, LANES), jnp.int32),
            pltpu.SemaphoreType.DMA((14,)),
        ],
        name="rim",
    )(*fields)
    up = [(i, (i + 1) % ny) for i in range(ny)]
    down = [((i + 1) % ny, i) for i in range(ny)]
    from_low = lax.ppermute(high, "gy", up)
    from_high = lax.ppermute(low, "gy", down)
    planes, west, east = pl.pallas_call(
        lambda *a: plane_kernel(rows, total_rows, *a),
        out_shape=(
            shape(NP, rows, LANES), shape(half + SUB, LANES), shape(half + SUB, LANES),
        ),
        in_specs=[VMEM] * 7 + [SMEM],
        out_specs=(VMEM, VMEM, VMEM),
        compiler_params=params(),
        name="planes",
    )(*fields)
    strip_spec = pl.BlockSpec((strip, LANES), lambda i: (0, 0))
    corner = pl.BlockSpec((SUB, LANES), lambda i: (half // SUB, 0))
    west, east = pl.pallas_call(
        corner_kernel,
        grid=(1,),
        out_shape=(shape(half + SUB, LANES),) * 2,
        in_specs=[strip_spec, strip_spec, ANY, ANY],
        out_specs=(corner, corner),
        input_output_aliases={2: 0, 3: 1},
        name="corners",
    )(from_low, from_high, west, east)
    right = [(i, (i + 1) % nx) for i in range(nx)]
    left = [((i + 1) % nx, i) for i in range(nx)]
    from_west = lax.ppermute(east, "gx", right)
    from_east = lax.ppermute(west, "gx", left)
    tall = ext + 2 * SUB
    basis, faces, partial = pl.pallas_call(
        lambda *a: solve_kernel(rows, *a),
        out_shape=(
            shape(ITERS + 1, 2, ext, LANES), shape(4, rows, LANES), shape(nx * ny, LANES),
        ),
        in_specs=[VMEM] * 5,
        out_specs=(VMEM, VMEM, VMEM),
        scratch_shapes=[
            pltpu.VMEM((NP, 2, tall, LANES), f32),
            pltpu.VMEM((2, tall, LANES), f32),
            pltpu.VMEM((2, tall, LANES), f32),
            pltpu.VMEM((2, tall, LANES), f32),
            pltpu.VMEM((2, tall, LANES), f32),
            pltpu.VMEM((ITERS, 2, tall, LANES), f32),
            pltpu.VMEM((4, 2, tall, LANES), f32),
            pltpu.VMEM((tall, LANES), f32),
        ],
        compiler_params=params(),
        name="solve",
    )(planes, from_low, from_high, from_west, from_east)
    parts = lax.all_to_all(partial, ("gx", "gy"), 0, 0, tiled=True)
    return pl.pallas_call(
        lambda *a: finish_kernel(rows, total_rows, *a),
        out_shape=(shape(levels, rows, LANES),) * 3 + (shape(rows, LANES),),
        in_specs=[VMEM] * 4 + [SMEM] + [VMEM] * 7,
        out_specs=(VMEM,) * 4,
        scratch_shapes=[pltpu.VMEM((2, ext, LANES), f32)],
        compiler_params=params(),
        name="finish",
    )(
        velocity_u, velocity_v, tracer, land_mask, clinic_map, parts, basis, faces, from_low,
        from_high, from_west, from_east,
    )


def solution(mesh):
    in_specs = (
        P(None, "gy", "gx"),
        P(None, "gy", "gx"),
        P(None, "gy", "gx"),
        P("gy", "gx"),
        P("gy", "gx"),
        P("gy", "gx"),
        P("gy", "gx"),
        P(),
        P(),
    )
    out_specs = (P(None, "gy", "gx"), P(None, "gy", "gx"), P(None, "gy", "gx"), P("gy", "gx"))
    return jax.shard_map(
        on_device, mesh=mesh, in_specs=in_specs, out_specs=out_specs, check_vma=False
    )
```

time: 436 us -> 52.8 us (0.12)
  blocking collectives: 274 us -> 0 us
  other arithmetic: 50.1 us -> 0 us
  waiting for transfers between devices: 44.9 us -> 10.5 us
  starting transfers between devices: 32.1 us -> 13.2 us
  Pallas kernels: 0 us -> 14.6 us
  between operations: 10.5 us -> 0.76 us
  local copies, waits for them, and re-layouts: 22 us -> 13 us
    psum x7 -> x0, blocking collectives: 274 us -> none  [the longest x4 163 us: norm_total(): return lax.psum(jnp.sum(residual * precond), ('gx', 'gy'))]
    ppermute x27 -> x4, waiting for transfers between devices: 44.9 us -> 3.5 us  [the longest x1 2.88 us: on_device(): from_west = lax.ppermute(east, 'gx', right)]
    ppermute x27 -> x4, starting transfers between devices: 32.1 us -> 7.83 us  [the longest x1 3.04 us: on_device(): from_east = lax.ppermute(west, 'gx', left)]
    reduce_sum x7 -> x0, other arithmetic: 22.8 us -> none  [the longest x1 8.33 us: on_device(): east_flow = wet_cycle * jnp.sum(thick * u_star, 0)]
    pallas_call x0 -> x5, Pallas kernels: none -> 14.6 us  [the longest x1 4.39 us: on_device(): pl.pallas_call(lambda *a: finish_kernel(rows, total_rows, *a), out_shape=...]
    add x7 -> x0, other arithmetic: 11.8 us -> none  [the longest x1 4.32 us: on_device(): t_new = keep_mask * tracer_raw + (1.0 - active) * tracer]
    all_to_all x0 -> x1, waiting for transfers between devices: none -> 7.02 us  [on_device(): parts = lax.all_to_all(partial, ('gx', 'gy'), 0, 0, tiled=True)]
    all_to_all x0 -> x1, starting transfers between devices: none -> 5.35 us  [on_device(): parts = lax.all_to_all(partial, ('gx', 'gy'), 0, 0, tiled=True)]
  transfers between devices with their start and end apart: 27 -> 5, of which waited for: 18 -> 3; matrix products, arithmetic and copies ran while one was open for 7% -> 0% of each run, Pallas kernels for 0% -> 5%
where the time goes in v1:
time: 52.8 us; the launch traced here: 52.1 us
  Pallas kernels  14.6 us (28%)
  starting transfers between devices  13.2 us (25%)
  local copies, waits for them, and re-layouts  13 us (25%)
  waiting for transfers between devices  10.5 us (20%)
  between operations  0.76 us (1%)
    unnamed x44, local copies, waits for them, and re-layouts  13 us
    all_to_all x1, waiting for transfers between devices, on_device(): parts = lax.all_to_all(partial, ('gx', 'gy'), 0, 0, tiled=True)  7.02 us
    all_to_all x1, starting transfers between devices, on_device(): parts = lax.all_to_all(partial, ('gx', 'gy'), 0, 0, tiled=True)  5.35 us
    pallas_call x1, Pallas kernels, on_device(): pl.pallas_call(lambda *a: finish_kernel(rows, total_rows, *a), out_shape=...  4.39 us
    pallas_call x1, Pallas kernels, on_device(): pl.pallas_call(lambda *a: solve_kernel(rows, *a), out_shape=(shape(ITERS...  3.26 us
    ppermute x1, starting transfers between devices, on_device(): from_east = lax.ppermute(west, 'gx', left)  3.04 us
    ppermute x1, waiting for transfers between devices, on_device(): from_west = lax.ppermute(east, 'gx', right)  2.88 us
    pallas_call x1, Pallas kernels, on_device(): pl.pallas_call(lambda *a: plane_kernel(rows, total_rows, *a), out_shape=(...  2.79 us
  transfers between devices with their start and end apart: 5, of which 3 were waited for; matrix products, arithmetic and copies ran while one was open for 0% of the time, Pallas kernels for 5%

profile of v1, /device:TPU:0, one launch (start us, length us, event | category | flops | bytes accessed | tf_op | source)
XLA Modules:
  0.0 52.1 jit_solution(4103963398009183026)
XLA Ops:
  0.6 0.0 copy-start.5
  0.6 0.0 copy-start.2
  0.7 0.0 copy-start.1
  0.7 0.0 copy-start
  0.7 0.0 copy-start.6
  0.7 1.5 %copy.18.a_7_ = s32[32,8]{1,0:T(8,128)} copy(s32[32,8]{0,1:T(8,128)} %param.17) | data formatting | bytes 2048 | tf_op args[8]
  2.2 0.0 copy-start.17
  2.2 2.7 %rim.1 = (f32[72,128]{1,0:T(8,128)}, f32[72,128]{1,0:T(8,128)}) custom-call(f32[4,320,128]{2,1,0:T(8,128)} %a_0_.5, f32[4,320,128]{2,1,0:T(8,128)} %a_1_.5, f32[4,320,128]{2,1,0:T(8,128)} %a_2_.5, f32[320,128]{1,0:T(8,128)} %a_3_.4, f32[320,128]{1,0:T(8,128)} %a_4_.4, f32[320,128]{1,0:T(8,128)} %a_5_.3, s32[320,128]{1,0:T(8,128)} %a_3_.5, s32[32,8]{1,0:T(8,128)} %copy.18.a_7_), custom_call_target="tpu_custom_call" | custom-call | tf_op jit(solution)/shard_map/rim/pallas_call | solution.py:510
  4.9 0.5 %collective-permute-start = (f32[72,128]{1,0:T(8,128)}, f32[72,128]{1,0:T(8,128)S(1)}, u32[]{:S(2)}, u32[]{:S(2)}) collective-permute-start(f32[72,128]{1,0:T(8,128)} %get-tuple-element.15), channel_id=1, source_target_pairs={{0,1},{1,2},{2,3},{3,0},{4,5},{5,6},{6,7},{7,4},{8,9},{9,10},{10,1... | collective-permute-start | bytes 110600 | tf_op jit(solution)/shard_map/ppermute | solution.py:525
  5.4 2.0 %collective-permute-start.1 = (f32[72,128]{1,0:T(8,128)}, f32[72,128]{1,0:T(8,128)S(1)}, u32[]{:S(2)}, u32[]{:S(2)}) collective-permute-start(f32[72,128]{1,0:T(8,128)} %get-tuple-element.16), channel_id=1, source_target_pairs={{1,0},{2,1},{3,2},{0,3},{5,4},{6,5},{7,6},{4,7},{9,8},{10,9},{11,1... | collective-permute-start | bytes 110600 | tf_op jit(solution)/shard_map/ppermute | solution.py:526
  7.4 0.0 copy-done.5
  7.4 0.0 copy-done.2
  7.4 0.0 copy-done.1
  7.4 0.0 copy-done
  7.4 0.0 copy-done.6
  7.5 0.0 copy-done.17
  7.5 0.0 copy-start.7
  7.5 0.9 %copy-done.7 = f32[320,128]{1,0:T(8,128)S(1)} copy-done((f32[320,128]{1,0:T(8,128)S(1)}, f32[320,128]{1,0:T(8,128)}, u32[]{:S(2)}) %copy-start.7) | copy-done | bytes 163864
  8.4 0.0 copy-start.8
  8.4 0.9 %copy-done.8 = f32[320,128]{1,0:T(8,128)S(1)} copy-done((f32[320,128]{1,0:T(8,128)S(1)}, f32[320,128]{1,0:T(8,128)}, u32[]{:S(2)}) %copy-start.8) | copy-done | bytes 163864
  9.3 0.0 copy-start.20
  9.3 2.8 %planes.1 = (f32[7,320,128]{2,1,0:T(8,128)S(1)}, f32[168,128]{1,0:T(8,128)S(1)}, f32[168,128]{1,0:T(8,128)S(1)}) custom-call(f32[4,320,128]{2,1,0:T(8,128)S(1)} %copy-done, f32[4,320,128]{2,1,0:T(8,128)S(1)} %copy-done.1, f32[4,320,128]{2,1,0:T(8,128)S(1)} %copy-done.2, f32[320,128]{1,0:T(8,128)S(1)} %copy-done.6, f32[320,128]{1,0:T(8,128)S(1)} %copy-done.7, ...), custom_call_target="tpu_custom_call" | custom-call | tf_op jit(solution)/shard_map/planes/pallas_call | solution.py:527
  12.1 0.0 copy-start.19
  12.1 0.6 %copy-done.19 = f32[168,128]{1,0:T(8,128)} copy-done((f32[168,128]{1,0:T(8,128)}, f32[168,128]{1,0:T(8,128)S(1)}, u32[]{:S(2)}) %copy-start.19) | copy-done | bytes 86040
  12.7 0.0 copy-start.18
  12.7 0.0 collective-permute-done.from_low.a_1_.a_8_
  12.7 0.0 copy-start.11
  12.7 0.0 collective-permute-done.1.from_high.a_2_.a_9_
  12.7 0.6 %copy-done.18 = f32[168,128]{1,0:T(8,128)} copy-done((f32[168,128]{1,0:T(8,128)}, f32[168,128]{1,0:T(8,128)S(1)}, u32[]{:S(2)}) %copy-start.18) | copy-done | bytes 86040
  13.4 0.0 copy-start.14
  13.4 0.0 copy-done.11
  13.4 0.6 %copy-done.14 = f32[72,128]{1,0:T(8,128)} copy-done((f32[72,128]{1,0:T(8,128)}, f32[72,128]{1,0:T(8,128)S(1)}, u32[]{:S(2)}) %copy-start.14) | copy-done | bytes 36888
  14.0 1.5 %corners.1 = (f32[168,128]{1,0:T(8,128)}, f32[168,128]{1,0:T(8,128)}) custom-call(f32[72,128]{1,0:T(8,128)} %copy-done.11, f32[72,128]{1,0:T(8,128)} %copy-done.14, f32[168,128]{1,0:T(8,128)} %copy-done.18, f32[168,128]{1,0:T(8,128)} %copy-done.19), custom_call_target="tpu_custom_call", output_to_operand_aliasing={{0}: (2, {}), {1}: (3, {})} | custom-call | tf_op jit(solution)/shard_map/corners/pallas_call | solution.py:539
  15.5 2.3 %collective-permute-start.2 = (f32[168,128]{1,0:T(8,128)}, f32[168,128]{1,0:T(8,128)S(1)}, u32[]{:S(2)}, u32[]{:S(2)}) collective-permute-start(f32[168,128]{1,0:T(8,128)} %get-tuple-element.19), channel_id=1, source_target_pairs={{0,4},{4,8},{8,12},{12,16},{16,20},{20,24},{24,28},{28,0},{1,5},{5... | collective-permute-start | bytes 258056 | tf_op jit(solution)/shard_map/ppermute | solution.py:550
  17.7 3.0 %collective-permute-start.3 = (f32[168,128]{1,0:T(8,128)}, f32[168,128]{1,0:T(8,128)S(1)}, u32[]{:S(2)}, u32[]{:S(2)}) collective-permute-start(f32[168,128]{1,0:T(8,128)} %get-tuple-element.20), channel_id=1, source_target_pairs={{4,0},{8,4},{12,8},{16,12},{20,16},{24,20},{28,24},{0,28},{5,1},{9... | collective-permute-start | bytes 258056 | tf_op jit(solution)/shard_map/ppermute | solution.py:551
  20.8 2.9 %collective-permute-done.2.a_3_.a_10_ = f32[168,128]{1,0:T(8,128)S(1)} collective-permute-done((f32[168,128]{1,0:T(8,128)}, f32[168,128]{1,0:T(8,128)S(1)}, u32[]{:S(2)}, u32[]{:S(2)}) %collective-permute-start.2) | collective-permute-done | bytes 86048 | tf_op jit(solution)/shard_map/ppermute | solution.py:550
  23.7 0.6 %collective-permute-done.3.a_4_.a_11_ = f32[168,128]{1,0:T(8,128)S(1)} collective-permute-done((f32[168,128]{1,0:T(8,128)}, f32[168,128]{1,0:T(8,128)S(1)}, u32[]{:S(2)}, u32[]{:S(2)}) %collective-permute-start.3) | collective-permute-done | bytes 86048 | tf_op jit(solution)/shard_map/ppermute | solution.py:551
  24.3 0.0 copy-start.12
  24.3 0.8 %copy-done.12 = f32[72,128]{1,0:T(8,128)S(1)} copy-done((f32[72,128]{1,0:T(8,128)S(1)}, f32[72,128]{1,0:T(8,128)}, u32[]{:S(2)}) %copy-start.12) | copy-done | bytes 36888
  25.0 0.0 copy-start.15
  25.0 0.8 %copy-done.15 = f32[72,128]{1,0:T(8,128)S(1)} copy-done((f32[72,128]{1,0:T(8,128)S(1)}, f32[72,128]{1,0:T(8,128)}, u32[]{:S(2)}) %copy-start.15) | copy-done | bytes 36888
  25.8 3.3 %solve.1 = (f32[5,2,336,128]{3,2,1,0:T(8,128)S(1)}, f32[4,320,128]{2,1,0:T(8,128)S(1)}, f32[32,128]{1,0:T(8,128)}) custom-call(f32[7,320,128]{2,1,0:T(8,128)S(1)} %get-tuple-element.14.a_0_, f32[72,128]{1,0:T(8,128)S(1)} %copy-done.12, f32[72,128]{1,0:T(8,128)S(1)} %copy-done.15, f32[168,128]{1,0:T(8,128)S(1)} %collective-permute-done.2.a_3_.a_10_, ...), custom_call_target="tpu_custom_call" | custom-call | tf_op jit(solution)/shard_map/solve/pallas_call | solution.py:553
  29.1 0.0 copy-start.3
  29.1 1.2 %copy-done.3 = f32[5,2,336,128]{3,2,1,0:T(8,128)} copy-done((f32[5,2,336,128]{3,2,1,0:T(8,128)}, f32[5,2,336,128]{3,2,1,0:T(8,128)S(1)}, u32[]{:S(2)}) %copy-start.3) | copy-done | bytes 1720344
  30.3 0.0 copy-start.9
  30.3 0.8 %copy-done.9 = f32[4,320,128]{2,1,0:T(8,128)} copy-done((f32[4,320,128]{2,1,0:T(8,128)}, f32[4,320,128]{2,1,0:T(8,128)S(1)}, u32[]{:S(2)}) %copy-start.9) | copy-done | bytes 655384
  31.1 5.3 %all-to-all-start = ((f32[32,1,128]{2,1,0:T(1,128)}), f32[32,1,128]{2,1,0:T(1,128)S(1)}, u32[]{:S(2)}, u32[]{:S(2)}) async-start(f32[32,1,128]{2,1,0:T(1,128)} %bitcast.1), calls=%async_computation | async-start | bytes 32768 | tf_op jit(solution)/shard_map/all_to_all | solution.py:573
  36.5 0.0 copy-done.20
  36.5 0.1 copy.21.a_4_
  36.6 7.0 %all-to-all-done = f32[32,1,128]{2,1,0:T(1,128)S(1)} async-done(((f32[32,1,128]{2,1,0:T(1,128)}), f32[32,1,128]{2,1,0:T(1,128)S(1)}, u32[]{:S(2)}, u32[]{:S(2)}) %all-to-all-start) | async-done | bytes 16416 | tf_op jit(solution)/shard_map/all_to_all | solution.py:573
  43.6 0.0 copy-start.4
  43.6 1.5 %copy-done.4 = f32[5,2,336,128]{3,2,1,0:T(8,128)S(1)} copy-done((f32[5,2,336,128]{3,2,1,0:T(8,128)S(1)}, f32[5,2,336,128]{3,2,1,0:T(8,128)}, u32[]{:S(2)}) %copy-start.4) | copy-done | bytes 1720344
  45.1 0.0 copy-start.10
  45.1 1.1 %copy-done.10 = f32[4,320,128]{2,1,0:T(8,128)S(1)} copy-done((f32[4,320,128]{2,1,0:T(8,128)S(1)}, f32[4,320,128]{2,1,0:T(8,128)}, u32[]{:S(2)}) %copy-start.10) | copy-done | bytes 655384
  46.2 0.0 copy-start.13
  46.2 0.8 %copy-done.13 = f32[72,128]{1,0:T(8,128)S(1)} copy-done((f32[72,128]{1,0:T(8,128)S(1)}, f32[72,128]{1,0:T(8,128)}, u32[]{:S(2)}) %copy-start.13) | copy-done | bytes 36888
  46.9 0.0 copy-start.16
  46.9 0.8 %copy-done.16 = f32[72,128]{1,0:T(8,128)S(1)} copy-done((f32[72,128]{1,0:T(8,128)S(1)}, f32[72,128]{1,0:T(8,128)}, u32[]{:S(2)}) %copy-start.16) | copy-done | bytes 36888
  47.7 4.4 %finish.1 = (f32[4,320,128]{2,1,0:T(8,128)}, f32[4,320,128]{2,1,0:T(8,128)}, f32[4,320,128]{2,1,0:T(8,128)}, f32[320,128]{1,0:T(8,128)}) custom-call(f32[4,320,128]{2,1,0:T(8,128)S(1)} %copy-done, f32[4,320,128]{2,1,0:T(8,128)S(1)} %copy-done.1, f32[4,320,128]{2,1,0:T(8,128)S(1)} %copy-done.2, s32[320,128]{1,0:T(8,128)S(1)} %copy-done.5, ...), custom_call_target="tpu_custom_call" | custom-call | tf_op jit(solution)/shard_map/finish/pallas_call | solution.py:574
Async XLA Ops:
  0.6 6.8 %copy-start.5 = (s32[320,128]{1,0:T(8,128)S(1)}, s32[320,128]{1,0:T(8,128)}, u32[]{:S(2)}) copy-start(s32[320,128]{1,0:T(8,128)} %a_3_.5) | copy-start | bytes 491524
  0.6 6.8 %copy-start.2 = (f32[4,320,128]{2,1,0:T(8,128)S(1)}, f32[4,320,128]{2,1,0:T(8,128)}, u32[]{:S(2)}) copy-start(f32[4,320,128]{2,1,0:T(8,128)} %a_2_.5) | copy-start | bytes 1966084
  0.7 6.8 %copy-start.1 = (f32[4,320,128]{2,1,0:T(8,128)S(1)}, f32[4,320,128]{2,1,0:T(8,128)}, u32[]{:S(2)}) copy-start(f32[4,320,128]{2,1,0:T(8,128)} %a_1_.5) | copy-start | bytes 1966084
  0.7 6.8 %copy-start = (f32[4,320,128]{2,1,0:T(8,128)S(1)}, f32[4,320,128]{2,1,0:T(8,128)}, u32[]{:S(2)}) copy-start(f32[4,320,128]{2,1,0:T(8,128)} %a_0_.5) | copy-start | bytes 1966084
  0.7 6.8 %copy-start.6 = (f32[320,128]{1,0:T(8,128)S(1)}, f32[320,128]{1,0:T(8,128)}, u32[]{:S(2)}) copy-start(f32[320,128]{1,0:T(8,128)} %a_3_.4) | copy-start | bytes 491524
  2.2 5.2 %copy-start.17 = (s32[32,8]{1,0:T(8,128)S(1)}, s32[32,8]{1,0:T(8,128)}, u32[]{:S(2)}) copy-start(s32[32,8]{1,0:T(8,128)} %copy.18.a_7_) | copy-start | bytes 3076
  4.9 7.8 %collective-permute-start = (f32[72,128]{1,0:T(8,128)}, f32[72,128]{1,0:T(8,128)S(1)}, u32[]{:S(2)}, u32[]{:S(2)}) collective-permute-start(f32[72,128]{1,0:T(8,128)} %get-tuple-element.15), channel_id=1, source_target_pairs={{0,1},{1,2},{2,3},{3,0},{4,5},{5,6},{6,7},{7,4},{8,9},{9,10},{10,1... | collective-permute-start | bytes 110600 | tf_op jit(solution)/shard_map/ppermute | solution.py:525
  5.4 7.3 %collective-permute-start.1 = (f32[72,128]{1,0:T(8,128)}, f32[72,128]{1,0:T(8,128)S(1)}, u32[]{:S(2)}, u32[]{:S(2)}) collective-permute-start(f32[72,128]{1,0:T(8,128)} %get-tuple-element.16), channel_id=1, source_target_pairs={{1,0},{2,1},{3,2},{0,3},{5,4},{6,5},{7,6},{4,7},{9,8},{10,9},{11,1... | collective-permute-start | bytes 110600 | tf_op jit(solution)/shard_map/ppermute | solution.py:526
  7.5 0.9 %copy-start.7 = (f32[320,128]{1,0:T(8,128)S(1)}, f32[320,128]{1,0:T(8,128)}, u32[]{:S(2)}) copy-start(f32[320,128]{1,0:T(8,128)} %a_4_.4) | copy-start | bytes 491524
  8.4 0.9 %copy-start.8 = (f32[320,128]{1,0:T(8,128)S(1)}, f32[320,128]{1,0:T(8,128)}, u32[]{:S(2)}) copy-start(f32[320,128]{1,0:T(8,128)} %a_5_.3) | copy-start | bytes 491524
  9.3 27.2 %copy-start.20 = (s32[32,8]{0,1:T(8,128)S(1)}, s32[32,8]{0,1:T(8,128)}, u32[]{:S(2)}) copy-start(s32[32,8]{0,1:T(8,128)} %param.16) | copy-start | bytes 3076
  12.1 0.6 %copy-start.19 = (f32[168,128]{1,0:T(8,128)}, f32[168,128]{1,0:T(8,128)S(1)}, u32[]{:S(2)}) copy-start(f32[168,128]{1,0:T(8,128)S(1)} %get-tuple-element.18.east_in) | copy-start | bytes 258052
  12.7 0.6 %copy-start.18 = (f32[168,128]{1,0:T(8,128)}, f32[168,128]{1,0:T(8,128)S(1)}, u32[]{:S(2)}) copy-start(f32[168,128]{1,0:T(8,128)S(1)} %get-tuple-element.17.west_in) | copy-start | bytes 258052
  12.7 0.6 %copy-start.11 = (f32[72,128]{1,0:T(8,128)}, f32[72,128]{1,0:T(8,128)S(1)}, u32[]{:S(2)}) copy-start(f32[72,128]{1,0:T(8,128)S(1)} %collective-permute-done.from_low.a_1_.a_8_) | copy-start | bytes 110596
  13.4 0.6 %copy-start.14 = (f32[72,128]{1,0:T(8,128)}, f32[72,128]{1,0:T(8,128)S(1)}, u32[]{:S(2)}) copy-start(f32[72,128]{1,0:T(8,128)S(1)} %collective-permute-done.1.from_high.a_2_.a_9_) | copy-start | bytes 110596
  15.5 8.2 %collective-permute-start.2 = (f32[168,128]{1,0:T(8,128)}, f32[168,128]{1,0:T(8,128)S(1)}, u32[]{:S(2)}, u32[]{:S(2)}) collective-permute-start(f32[168,128]{1,0:T(8,128)} %get-tuple-element.19), channel_id=1, source_target_pairs={{0,4},{4,8},{8,12},{12,16},{16,20},{20,24},{24,28},{28,0},{1,5},{5... | collective-permute-start | bytes 258056 | tf_op jit(solution)/shard_map/ppermute | solution.py:550
  17.7 6.5 %collective-permute-start.3 = (f32[168,128]{1,0:T(8,128)}, f32[168,128]{1,0:T(8,128)S(1)}, u32[]{:S(2)}, u32[]{:S(2)}) collective-permute-start(f32[168,128]{1,0:T(8,128)} %get-tuple-element.20), channel_id=1, source_target_pairs={{4,0},{8,4},{12,8},{16,12},{20,16},{24,20},{28,24},{0,28},{5,1},{9... | collective-permute-start | bytes 258056 | tf_op jit(solution)/shard_map/ppermute | solution.py:551
  24.3 0.8 %copy-start.12 = (f32[72,128]{1,0:T(8,128)S(1)}, f32[72,128]{1,0:T(8,128)}, u32[]{:S(2)}) copy-start(f32[72,128]{1,0:T(8,128)} %copy-done.11) | copy-start | bytes 110596
  25.0 0.8 %copy-start.15 = (f32[72,128]{1,0:T(8,128)S(1)}, f32[72,128]{1,0:T(8,128)}, u32[]{:S(2)}) copy-start(f32[72,128]{1,0:T(8,128)} %copy-done.14) | copy-start | bytes 110596
  29.1 1.2 %copy-start.3 = (f32[5,2,336,128]{3,2,1,0:T(8,128)}, f32[5,2,336,128]{3,2,1,0:T(8,128)S(1)}, u32[]{:S(2)}) copy-start(f32[5,2,336,128]{3,2,1,0:T(8,128)S(1)} %get-tuple-element.22.a_6_) | copy-start | bytes 5160964
  30.3 0.8 %copy-start.9 = (f32[4,320,128]{2,1,0:T(8,128)}, f32[4,320,128]{2,1,0:T(8,128)S(1)}, u32[]{:S(2)}) copy-start(f32[4,320,128]{2,1,0:T(8,128)S(1)} %get-tuple-element.23.a_7_) | copy-start | bytes 1966084
  31.1 12.5 %all-to-all-start = ((f32[32,1,128]{2,1,0:T(1,128)}), f32[32,1,128]{2,1,0:T(1,128)S(1)}, u32[]{:S(2)}, u32[]{:S(2)}) async-start(f32[32,1,128]{2,1,0:T(1,128)} %bitcast.1), calls=%async_computation | async-start | bytes 32768 | tf_op jit(solution)/shard_map/all_to_all | solution.py:573
  43.6 1.5 %copy-start.4 = (f32[5,2,336,128]{3,2,1,0:T(8,128)S(1)}, f32[5,2,336,128]{3,2,1,0:T(8,128)}, u32[]{:S(2)}) copy-start(f32[5,2,336,128]{3,2,1,0:T(8,128)} %copy-done.3) | copy-start | bytes 5160964
  45.1 1.1 %copy-start.10 = (f32[4,320,128]{2,1,0:T(8,128)S(1)}, f32[4,320,128]{2,1,0:T(8,128)}, u32[]{:S(2)}) copy-start(f32[4,320,128]{2,1,0:T(8,128)} %copy-done.9) | copy-start | bytes 1966084
  46.2 0.8 %copy-start.13 = (f32[72,128]{1,0:T(8,128)S(1)}, f32[72,128]{1,0:T(8,128)}, u32[]{:S(2)}) copy-start(f32[72,128]{1,0:T(8,128)} %copy-done.11) | copy-start | bytes 110596
  46.9 0.8 %copy-start.16 = (f32[72,128]{1,0:T(8,128)S(1)}, f32[72,128]{1,0:T(8,128)}, u32[]{:S(2)}) copy-start(f32[72,128]{1,0:T(8,128)} %copy-done.14) | copy-start | bytes 110596

commit v2 on v1

--- a/solution.py
+++ b/solution.py
@@ -23,6 +23,8 @@
 OFFSETS = tuple(sum(WIDTHS[:i]) for i in range(len(WIDTHS)))
 EDGE = sum(WIDTHS)
 NP = len(PLANES)
+WET = PLANES.index("wet")
+OTHERS = tuple(i for i in range(NP) if i != WET)
 f32 = jnp.float32
 
 
@@ -74,7 +76,7 @@
 
 def domain_at(tropic_ref, row_dev, col_dev, rows, row):
     block = row_dev * (rows // BY) + row // BY
-    return jnp.where(tropic_ref[block, col_dev] >= 0, 1.0, 0.0).astype(f32)
+    return jnp.where(tropic_ref[col_dev, block] >= 0, 1.0, 0.0).astype(f32)
 
 
 def rim_kernel(
@@ -130,7 +132,9 @@
     return out
 
 
-def plane_kernel(rows, total_rows, u, v, t, p, depth, helm, land, tropic, planes, west, east):
+def plane_kernel(
+    rows, total_rows, u, v, t, p, depth, helm, land, tropic, planes, wet, west, east, u_copy, v_copy
+):
     col_dev, row_dev = place()
     levels = u.shape[0]
     half = rows // 2
@@ -146,8 +150,12 @@
             us, vs, p[here, :], depth[here, :], helm[here, :], land[here, :], domain,
             row_dev * rows + r, total_rows,
         )
-        for i, plane in enumerate(out):
-            planes[i, here, :] = plane
+        for i, plane in zip(OTHERS, range(NP - 1)):
+            planes[plane, here, :] = out[i]
+        wet[here, :] = out[WET]
+        for k in range(levels):
+            u_copy[k, here, :] = us[k]
+            v_copy[k, here, :] = vs[k]
         return out, us + vs + ts
 
     unroll = 4
@@ -187,8 +195,8 @@
 
 
 def solve_kernel(
-    rows, planes, from_low, from_high, from_west, from_east,
-    basis, faces, partial, F, face_e, face_n, flow_e, flow_n, T, coef, diag,
+    rows, planes, wet_in, from_low, from_high, from_west, from_east,
+    basis, edge, partial, F, face_e, face_n, flow_e, flow_n, T, coef, diag,
 ):
     ext = rows + 2 * SUB
     half = rows // 2
@@ -218,7 +226,7 @@
     for i in range(NP):
         F[i, 0, pl.ds(SUB, SUB), :] = from_low[pl.ds(SUB * i, SUB), :]
         F[i, 0, pl.ds(SUB + SUB + rows, SUB), :] = from_high[pl.ds(SUB * i, SUB), :]
-        F[i, 0, pl.ds(2 * SUB, rows), :] = planes[i]
+        F[i, 0, pl.ds(2 * SUB, rows), :] = wet_in[...] if i == WET else planes[OTHERS.index(i)]
     unpack(pl.ds(SUB, SUB), pl.ds(half, SUB), 0)
     unpack(pl.ds(2 * SUB + rows, SUB), pl.ds(half, SUB), HALF)
     step = 40
@@ -268,6 +276,10 @@
         lo, hi = max(r, 2 * SUB), min(r + CH, 2 * SUB + rows)
         return lo - r, hi - r
 
+    def keep_core(ref, i, r, value):
+        lo, hi = core_rows(r)
+        ref[i, r + lo - 2 * SUB : r + hi - 2 * SUB, :] = value[lo:hi]
+
     sums = [None] * (2 * ITERS)
 
     def add_sum(i, r, value):
@@ -284,7 +296,6 @@
         _, efw = shifted(*ef)
         nf, nfs = load(flow_n, (), r), load(flow_n, (), r, -1)
         x, e, w, n, s = around(F, (iS,), r)
-        lo, hi = core_rows(r)
         for c in both:
             mask = wet[c] > 0.0
             force = jnp.where(mask, -(ef[c] - efw[c]) - (nf[c] - nfs[c]), 0.0)
@@ -301,8 +312,8 @@
             if c == 0:
                 diag[here, :] = d
                 add_sum(0, r, res * z)
-                for i, f in enumerate((fe, fw, fn, fs)):
-                    faces[i, r + lo - 2 * SUB : r + hi - 2 * SUB, :] = f[0][lo:hi]
+                keep_core(basis, 0, r, x[0])
+                keep_core(basis, 1, r, z)
 
     def stage_step(k, r):
         x, e, w, n, s = around(T, (k,), r)
@@ -321,6 +332,7 @@
                 add_sum(2 * k + 1, r, d * x[c] * y)
                 if k + 1 < ITERS:
                     add_sum(2 * k + 2, r, d * y * y)
+                    keep_core(basis, k + 2, r, y)
 
     stages = [stage_faces, stage_flows, stage_residual]
     stages += [lambda r, k=k: stage_step(k, r) for k in range(ITERS)]
@@ -333,10 +345,24 @@
             if 0 <= i - lag < len(chunks):
                 stage(chunks[i - lag])
 
-    for c in both:
-        basis[0, c] = F[iS, c, SUB : SUB + ext, :]
-        for k in range(ITERS):
-            basis[k + 1, c] = T[k, c, SUB : SUB + ext, :]
+    vectors = [lambda c, here: F[iS, c, here, :]]
+    vectors += [lambda c, here, k=k: T[k, c, here, :] for k in range(ITERS)]
+    assert len(vectors) + 2 <= SUB
+    for r in range(0, rows, BY):
+        here = slice(2 * SUB + r, 2 * SUB + r + BY)
+        side = F[iW, 1, here, :]
+        lane = lane_of(side)
+        tile = jnp.where(lane == SUB, roll(side, SUB), 0.0)
+        tile = jnp.where(lane == SUB + 1, roll(side, SUB + 2), tile)
+        for j, get in enumerate(vectors):
+            tile = jnp.where(lane == j, roll(get(1, here), j), tile)
+        edge[r : r + BY, :] = tile
+    north = 2 * SUB + rows
+    edge[rows:, :] = jnp.zeros((SUB, LANES), f32)
+    for j, get in enumerate(vectors):
+        edge[rows + j : rows + j + 1, :] = get(0, slice(north, north + 1))
+    edge[rows + SUB - 2 : rows + SUB - 1, :] = F[iW, 0, north : north + 1, :]
+    edge[rows + SUB - 1 :, :] = F[iW, 0, 2 * SUB - 1 : 2 * SUB, :]
     lane = lax.broadcasted_iota(jnp.int32, (1, LANES), 1)
     line = jnp.zeros((1, LANES), f32)
     for i, total in enumerate(sums):
@@ -391,13 +417,97 @@
     return x
 
 
-def finish_kernel(
-    rows, total_rows, u, v, t, land, clinic, parts, basis, faces, from_low, from_high, from_west,
-    from_east, u_out, v_out, t_out, p_out, pres,
+def star_kernel(
+    rows, total_rows, u, v, t, land, clinic, wet, edge, from_low, from_high, from_west, from_east,
+    u_out, v_out, t_out,
 ):
     col_dev, row_dev = place()
     levels = u.shape[0]
     half = rows // 2
+    below = {}
+    for i, ref in enumerate((u, v, t)):
+        for k in range(levels):
+            n = SUB * NP + i * levels + k
+            below[i, k] = from_low[n : n + 1, :]
+    for r in range(0, rows, BY):
+        block = row_dev * (rows // BY) + r // BY
+        active = clinic[col_dev, block].astype(f32)
+        here = slice(r, r + BY)
+        keep = land[here, :].astype(f32) * active
+        rest = 1.0 - active
+        h = wet[here, :]
+        lane = lane_of(h)
+        first, last = lane == 0, lane == LANES - 1
+        beside = edge[here, :]
+        fe = jnp.minimum(h, jnp.where(last, roll(beside, LANES - 1 - SUB), roll(h, -1)))
+        fw = jnp.minimum(h, jnp.where(first, roll(beside, -(SUB + 1)), roll(h, 1)))
+        h_n = wet[r + 1 : r + BY + 1, :] if r + BY < rows else jnp.concatenate(
+            [h[1:], edge[rows + SUB - 2 : rows + SUB - 1, :]], 0
+        )
+        h_s = wet[r - 1 : r + BY - 1, :] if r > 0 else jnp.concatenate(
+            [edge[rows + SUB - 1 :, :], h[:-1]], 0
+        )
+        fn, fs = jnp.minimum(h, h_n), jnp.minimum(h, h_s)
+        row = row_dev * rows + r + lax.broadcasted_iota(jnp.int32, (BY, LANES), 0)
+        coriolis = 0.2 + 0.6 * ((row.astype(f32) + 0.5) / total_rows)
+        src = slice(r % half, r % half + BY)
+        base = HALF * (r // half) + EDGE
+        now = {(i, k): ref[k, here, :] for i, ref in enumerate((u, v, t)) for k in range(levels)}
+
+        def around(ref, which, k):
+            i = SUB * NP + which * levels + k
+            a = now[which, k]
+            lo = base + which * levels + k
+            e = jnp.where(last, roll(from_east[src, :], LANES - 1 - lo), roll(a, -1))
+            w = jnp.where(first, roll(from_west[src, :], -lo), roll(a, 1))
+            if r + BY < rows:
+                n = ref[k, r + 1 : r + BY + 1, :]
+            else:
+                n = jnp.concatenate([a[1:], from_high[i : i + 1, :]], 0)
+            s = jnp.concatenate([below[which, k], a[:-1]], 0)
+            return a, e, w, n, s
+
+        def diffuse(a, e, w, n, s):
+            return fe * (e - a) + fw * (w - a) + fn * (n - a) + fs * (s - a)
+
+        def mixing(which, k, a):
+            total = None
+            if k + 1 < levels:
+                total = now[which, k + 1] - a
+            if k > 0:
+                down = a - now[which, k - 1]
+                total = -down if total is None else total - down
+            return jnp.zeros_like(a) if total is None else total
+
+        results = []
+        for k in range(levels):
+            ua = around(u, 0, k)
+            va = around(v, 1, k)
+            ta = around(t, 2, k)
+            uc, vc, tc = ua[0], va[0], ta[0]
+            u_star = uc + step_time * (
+                vertical * mixing(0, k, uc) + viscosity * diffuse(*ua) + coriolis * vc
+            )
+            v_star = vc + step_time * (
+                vertical * mixing(1, k, vc) + viscosity * diffuse(*va) - coriolis * uc
+            )
+            raw = tc + step_time * (
+                vertical * mixing(2, k, tc) + diffusivity * diffuse(*ta)
+                - 0.5 * (uc * (ta[1] - ta[2]) + vc * (ta[3] - ta[4]))
+            )
+            t_out[k, here, :] = keep * raw + rest * tc
+            results.append((keep * u_star + rest * uc, keep * v_star + rest * vc))
+        below = {key: a[BY - 1 :] for key, a in now.items()}
+        for k, (u_base, v_base) in enumerate(results):
+            u_out[k, here, :] = u_base
+            v_out[k, here, :] = v_base
+
+
+def finish_kernel(
+    rows, parts, basis, edge, land, clinic, u, v, u_out, v_out, p_out
+):
+    col_dev, row_dev = place()
+    levels = u.shape[0]
     lane1 = lax.broadcasted_iota(jnp.int32, (1, LANES), 1)
     line = jnp.sum(parts[...], axis=0, keepdims=True)
     sums = []
@@ -406,85 +516,41 @@
         sums.append(jnp.broadcast_to(one, (1, LANES)))
     m = sums[:2] + [2.0 * s - sums[i % 2] for i, s in enumerate(sums[2:])]
     x = coefficients(m)
-    ext = rows + 2 * SUB
-    for r in range(0, ext, CH):
-        here = slice(r, r + CH)
-        for c in range(2):
-            total = basis[0, c, here, :]
-            for k in range(ITERS):
-                total = total + x[k] * basis[k + 1, c, here, :]
-            pres[c, here, :] = total
+    weights = jnp.where(lane1 == 0, 1.0, 0.0)
+    for k in range(ITERS):
+        weights = jnp.where(lane1 == k + 1, x[k], weights)
+
+    def mix(rows_of):
+        total = rows_of(0)
+        for k in range(ITERS):
+            total = total + x[k] * rows_of(k + 1)
+        return total
 
     for r in range(0, rows, BY):
-        block = row_dev * (rows // BY) + r // BY
-        active = clinic[block, col_dev].astype(f32)
-        here = pl.ds(r, BY)
+        p_out[r : r + BY, :] = mix(lambda j: basis[j, r : r + BY, :])
+    above = mix(lambda j: edge[rows + j : rows + j + 1, :])
+    for r in range(0, rows, BY):
+        here = slice(r, r + BY)
+        p = p_out[here, :]
+        active = clinic[col_dev, row_dev * (rows // BY) + r // BY].astype(f32)
         keep = land[here, :].astype(f32) * active
-        rest = 1.0 - active
-        pc = pres[0, SUB + r : SUB + r + BY, :]
-        ph = pres[1, SUB + r : SUB + r + BY, :]
-        p_out[here, :] = pc
-        lane = lane_of(pc)
-        first, last = lane == 0, lane == LANES - 1
-        grad_x = jnp.where(last, roll(ph, -1), roll(pc, -1)) - pc
-        grad_y = pres[0, SUB + r + 1 : SUB + r + BY + 1, :] - pc
-        fe, fw, fn, fs = (faces[i, here, :] for i in range(4))
-        row = row_dev * rows + r + lax.broadcasted_iota(jnp.int32, (BY, LANES), 0)
-        coriolis = 0.2 + 0.6 * ((row.astype(f32) + 0.5) / total_rows)
-        src = pl.ds(r % half, BY)
-        base = HALF * (r // half) + EDGE
-
-        def around(ref, which, k):
-            n_row = SUB * NP + which * levels + k
-            a = ref[k, here, :]
-            lo = base + which * levels + k
-            e = jnp.where(last, roll(from_east[src, :], LANES - 1 - lo), roll(a, -1))
-            w = jnp.where(first, roll(from_west[src, :], -lo), roll(a, 1))
-            if r + BY < rows:
-                n = ref[k, r + 1 : r + BY + 1, :]
-            else:
-                n = jnp.concatenate([a[1:], from_high[n_row : n_row + 1, :]], 0)
-            if r > 0:
-                s = ref[k, r - 1 : r + BY - 1, :]
-            else:
-                s = jnp.concatenate([from_low[n_row : n_row + 1, :], a[:-1]], 0)
-            return a, e, w, n, s
-
-        def diffuse(a, e, w, n, s):
-            return fe * (e - a) + fw * (w - a) + fn * (n - a) + fs * (s - a)
-
-        def mixing(ref, k, a):
-            total = None
-            if k + 1 < levels:
-                total = ref[k + 1, here, :] - a
-            if k > 0:
-                down = a - ref[k - 1, here, :]
-                total = -down if total is None else total - down
-            return jnp.zeros_like(a) if total is None else total
-
+        side = jnp.sum(edge[here, :] * weights, axis=1, keepdims=True)
+        east = jnp.where(lane_of(p) == LANES - 1, side, roll(p, -1))
+        if r + BY < rows:
+            north = p_out[r + 1 : r + BY + 1, :]
+        else:
+            north = jnp.concatenate([p[1:], above], 0)
+        push_x = keep * (gravity * (east - p))
+        push_y = keep * (gravity * (north - p))
         for k in range(levels):
-            ua = around(u, 0, k)
-            va = around(v, 1, k)
-            ta = around(t, 2, k)
-            uc, vc, tc = ua[0], va[0], ta[0]
-            u_star = uc + step_time * (
-                vertical * mixing(u, k, uc) + viscosity * diffuse(*ua) + coriolis * vc
-            )
-            v_star = vc + step_time * (
-                vertical * mixing(v, k, vc) + viscosity * diffuse(*va) - coriolis * uc
-            )
-            raw = tc + step_time * (
-                vertical * mixing(t, k, tc) + diffusivity * diffuse(*ta)
-                - 0.5 * (uc * (ta[1] - ta[2]) + vc * (ta[3] - ta[4]))
-            )
-            u_out[k, here, :] = keep * (u_star - gravity * grad_x) + rest * uc
-            v_out[k, here, :] = keep * (v_star - gravity * grad_y) + rest * vc
-            t_out[k, here, :] = keep * raw + rest * tc
+            u_out[k, here, :] = u[k, here, :] - push_x
+            v_out[k, here, :] = v[k, here, :] - push_y
 
 
 VMEM = pl.BlockSpec(memory_space=pltpu.VMEM)
 SMEM = pl.BlockSpec(memory_space=pltpu.SMEM)
 ANY = pl.BlockSpec(memory_space=pl.ANY)
+HBM = pl.BlockSpec(memory_space=pltpu.HBM)
 
 
 def shape(*dims):
@@ -502,15 +568,15 @@
     half = rows // 2
     ext = rows + 2 * SUB
     strip = -(-(SUB * NP + 3 * levels) // SUB) * SUB
-    fields = (velocity_u, velocity_v, tracer, pressure_old, depth, helm, land_mask, tropic_map)
-
-    def params(**kw):
-        return pltpu.CompilerParams(vmem_limit_bytes=40 << 20, **kw)
+    fields = (velocity_u, velocity_v, tracer, pressure_old, depth, helm, land_mask, tropic_map.T)
+
+    def params(mib):
+        return pltpu.CompilerParams(vmem_limit_bytes=mib << 20)
 
     low, high = pl.pallas_call(
         lambda *a: rim_kernel(rows, total_rows, *a),
         out_shape=(shape(strip, LANES), shape(strip, LANES)),
-        in_specs=[ANY] * 7 + [SMEM],
+        in_specs=[HBM] * 7 + [SMEM],
         out_specs=(VMEM, VMEM),
         scratch_shapes=[
             pltpu.VMEM((2, 3, levels, SUB, LANES), f32),
@@ -518,20 +584,22 @@
             pltpu.VMEM((2, SUB, LANES), jnp.int32),
             pltpu.SemaphoreType.DMA((14,)),
         ],
+        compiler_params=params(58),
         name="rim",
     )(*fields)
     up = [(i, (i + 1) % ny) for i in range(ny)]
     down = [((i + 1) % ny, i) for i in range(ny)]
     from_low = lax.ppermute(high, "gy", up)
     from_high = lax.ppermute(low, "gy", down)
-    planes, west, east = pl.pallas_call(
+    planes, wet, west, east, u_copy, v_copy = pl.pallas_call(
         lambda *a: plane_kernel(rows, total_rows, *a),
         out_shape=(
-            shape(NP, rows, LANES), shape(half + SUB, LANES), shape(half + SUB, LANES),
+            shape(NP - 1, rows, LANES), shape(rows, LANES), shape(half + SUB, LANES),
+            shape(half + SUB, LANES), shape(levels, rows, LANES), shape(levels, rows, LANES),
         ),
         in_specs=[VMEM] * 7 + [SMEM],
-        out_specs=(VMEM, VMEM, VMEM),
-        compiler_params=params(),
+        out_specs=(VMEM,) * 6,
+        compiler_params=params(6),
         name="planes",
     )(*fields)
     strip_spec = pl.BlockSpec((strip, LANES), lambda i: (0, 0))
@@ -543,6 +611,7 @@
         in_specs=[strip_spec, strip_spec, ANY, ANY],
         out_specs=(corner, corner),
         input_output_aliases={2: 0, 3: 1},
+        compiler_params=params(2),
         name="corners",
     )(from_low, from_high, west, east)
     right = [(i, (i + 1) % nx) for i in range(nx)]
@@ -550,13 +619,14 @@
     from_west = lax.ppermute(east, "gx", right)
     from_east = lax.ppermute(west, "gx", left)
     tall = ext + 2 * SUB
-    basis, faces, partial = pl.pallas_call(
+    basis, edge, partial = pl.pallas_call(
         lambda *a: solve_kernel(rows, *a),
         out_shape=(
-            shape(ITERS + 1, 2, ext, LANES), shape(4, rows, LANES), shape(nx * ny, LANES),
+            shape(ITERS + 1, rows, LANES), shape(rows + SUB, LANES),
+            shape(nx * ny, LANES),
         ),
-        in_specs=[VMEM] * 5,
-        out_specs=(VMEM, VMEM, VMEM),
+        in_specs=[VMEM] * 6,
+        out_specs=(VMEM,) * 3,
         scratch_shapes=[
             pltpu.VMEM((NP, 2, tall, LANES), f32),
             pltpu.VMEM((2, tall, LANES), f32),
@@ -567,22 +637,33 @@
             pltpu.VMEM((4, 2, tall, LANES), f32),
             pltpu.VMEM((tall, LANES), f32),
         ],
-        compiler_params=params(),
+        compiler_params=params(12),
         name="solve",
-    )(planes, from_low, from_high, from_west, from_east)
+    )(planes, wet, from_low, from_high, from_west, from_east)
     parts = lax.all_to_all(partial, ("gx", "gy"), 0, 0, tiled=True)
-    return pl.pallas_call(
-        lambda *a: finish_kernel(rows, total_rows, *a),
-        out_shape=(shape(levels, rows, LANES),) * 3 + (shape(rows, LANES),),
-        in_specs=[VMEM] * 4 + [SMEM] + [VMEM] * 7,
-        out_specs=(VMEM,) * 4,
-        scratch_shapes=[pltpu.VMEM((2, ext, LANES), f32)],
-        compiler_params=params(),
+    full = levels * rows * LANES
+    u_base, v_base, t_new = pl.pallas_call(
+        lambda *a: star_kernel(rows, total_rows, *a),
+        out_shape=(shape(levels, rows, LANES),) * 3,
+        in_specs=[VMEM] * 4 + [SMEM] + [VMEM] * 6,
+        out_specs=(VMEM,) * 3,
+        input_output_aliases={0: 0, 1: 1},
+        compiler_params=params(8),
+        cost_estimate=pl.CostEstimate(flops=400 * full, bytes_accessed=24 * full, transcendentals=0),
+        name="star",
+    )(
+        u_copy, v_copy, tracer, land_mask, clinic_map.T, wet, edge, from_low, from_high,
+        from_west, from_east,
+    )
+    u_new, v_new, pressure = pl.pallas_call(
+        lambda *a: finish_kernel(rows, *a),
+        out_shape=(shape(levels, rows, LANES),) * 2 + (shape(rows, LANES),),
+        in_specs=[VMEM] * 4 + [SMEM] + [VMEM] * 2,
+        out_specs=(VMEM,) * 3,
+        compiler_params=params(4),
         name="finish",
-    )(
-        velocity_u, velocity_v, tracer, land_mask, clinic_map, parts, basis, faces, from_low,
-        from_high, from_west, from_east,
-    )
+    )(parts, basis, edge, land_mask, clinic_map.T, u_base, v_base)
+    return u_new, v_new, t_new, pressure
 
 
 def solution(mesh):

time: 52.8 us -> 35.5 us (0.67)
  local copies, waits for them, and re-layouts: 13 us -> 1.32 us
  waiting for transfers between devices: 10.5 us -> 6.39 us
  Pallas kernels: 14.6 us -> 13.9 us
    unnamed x44 -> x20, local copies, waits for them, and re-layouts: 13 us -> 1.32 us
    all_to_all x1, waiting for transfers between devices: 7.02 us -> 2.72 us  [on_device(): parts = lax.all_to_all(partial, ('gx', 'gy'), 0, 0, tiled=True)]
    pallas_call x1, Pallas kernels: 1.48 us -> 0.09 us  [on_device(): pl.pallas_call(corner_kernel, grid=(1,), out_shape=(shape(half + SUB, LAN...]
    pallas_call x1 -> x2, Pallas kernels: 4.39 us -> 5.73 us  [the longest x1 3.69 us: on_device(): pl.pallas_call(lambda *a: star_kernel(rows, total_rows, *a), out_shape=(s...]
  transfers between devices with their start and end apart: 5 -> 5, of which waited for: 3 -> 3; matrix products, arithmetic and copies ran while one was open for 0% -> 0% of each run, Pallas kernels for 5% -> 18%
where the time goes in v2:
time: 35.5 us; the launch traced here: 35.2 us
  Pallas kernels  13.9 us (39%)
  starting transfers between devices  12.9 us (36%)
  waiting for transfers between devices  6.39 us (18%)
  local copies, waits for them, and re-layouts  1.32 us (4%)
  between operations  0.8 us (2%)
    all_to_all x1, starting transfers between devices, on_device(): parts = lax.all_to_all(partial, ('gx', 'gy'), 0, 0, tiled=True)  4.92 us
    pallas_call x1, Pallas kernels, on_device(): pl.pallas_call(lambda *a: star_kernel(rows, total_rows, *a), out_shape=(s...  3.69 us
    ppermute x1, waiting for transfers between devices, on_device(): from_west = lax.ppermute(east, 'gx', right)  3.34 us
    ppermute x1, starting transfers between devices, on_device(): from_east = lax.ppermute(west, 'gx', left)  3.11 us
    pallas_call x1, Pallas kernels, on_device(): pl.pallas_call(lambda *a: solve_kernel(rows, *a), out_shape=(shape(ITERS...  2.95 us
    all_to_all x1, waiting for transfers between devices, on_device(): parts = lax.all_to_all(partial, ('gx', 'gy'), 0, 0, tiled=True)  2.72 us
    pallas_call x1, Pallas kernels, on_device(): pl.pallas_call(lambda *a: plane_kernel(rows, total_rows, *a), out_shape=(...  2.61 us
    pallas_call x1, Pallas kernels, on_device(): pl.pallas_call(lambda *a: rim_kernel(rows, total_rows, *a), out_shape=(sh...  2.49 us
  transfers between devices with their start and end apart: 5, of which 3 were waited for; matrix products, arithmetic and copies ran while one was open for 0% of the time, Pallas kernels for 18%

profile of v2, /device:TPU:0, one launch (start us, length us, event | category | flops | bytes accessed | tf_op | source)
XLA Modules:
  0.0 35.2 jit_solution(10894203075631426496)
XLA Ops:
  0.6 0.0 copy-start
  0.6 0.0 copy-start.1
  0.7 0.0 copy-start.2
  0.7 0.0 copy-start.3
  0.7 0.0 copy-start.4
  0.7 0.0 copy-start.5
  0.7 0.0 copy-start.6
  0.7 0.0 copy-start.7
  0.7 2.5 %rim.1 = (f32[72,128]{1,0:T(8,128)}, f32[72,128]{1,0:T(8,128)}) custom-call(f32[4,320,128]{2,1,0:T(8,128)} %a_0_.3, f32[4,320,128]{2,1,0:T(8,128)} %a_1_.3, f32[4,320,128]{2,1,0:T(8,128)} %a_2_.5, f32[320,128]{1,0:T(8,128)} %a_3_.5, f32[320,128]{1,0:T(8,128)} %a_4_.3, f32[320,128]{1,0:T(8,128)} %a_5_.3, s32[320,128]{1,0:T(8,128)} %a_3_.7, s32[8,32]{1,0:T(8,128)} %bitcast.7), custom_call_target="tpu_custom_call" | custom-call | tf_op jit(solution)/shard_map/rim/pallas_call | solution.py:576
  3.2 0.5 %collective-permute-start = (f32[72,128]{1,0:T(8,128)}, f32[72,128]{1,0:T(8,128)S(1)}, u32[]{:S(2)}, u32[]{:S(2)}) collective-permute-start(f32[72,128]{1,0:T(8,128)} %get-tuple-element.25), channel_id=1, source_target_pairs={{0,1},{1,2},{2,3},{3,0},{4,5},{5,6},{6,7},{7,4},{8,9},{9,10},{10,1... | collective-permute-start | bytes 110600 | tf_op jit(solution)/shard_map/ppermute | solution.py:592
  3.8 2.0 %collective-permute-start.1 = (f32[72,128]{1,0:T(8,128)}, f32[72,128]{1,0:T(8,128)S(1)}, u32[]{:S(2)}, u32[]{:S(2)}) collective-permute-start(f32[72,128]{1,0:T(8,128)} %get-tuple-element.26), channel_id=1, source_target_pairs={{1,0},{2,1},{3,2},{0,3},{5,4},{6,5},{7,6},{4,7},{9,8},{10,9},{11,1... | collective-permute-start | bytes 110600 | tf_op jit(solution)/shard_map/ppermute | solution.py:593
  5.7 0.0 copy-done
  5.7 0.0 copy-done.1
  5.7 0.0 copy-done.2
  5.7 0.0 copy-done.3
  5.7 0.0 copy-done.4
  5.8 0.0 copy-done.5
  5.8 0.0 copy-done.6
  5.8 0.0 copy-done.7
  5.8 2.6 %planes.1 = (f32[6,320,128]{2,1,0:T(8,128)S(1)}, f32[320,128]{1,0:T(8,128)S(1)}, f32[168,128]{1,0:T(8,128)S(1)}, f32[168,128]{1,0:T(8,128)S(1)}, f32[4,320,128]{2,1,0:T(8,128)S(1)}, /*index=5*/f32[4,320,128]{2,1,0:T(8,128)S(1)}) custom-call(f32[4,320,128]{2,1,0:T(8,128)S(1)} %copy-done.2, f32[4,320,128]{2,1,0:T(8,128)S(1)} %copy-done.3, ...), custom_call_target="tpu_custom_call" | custom-call | tf_op jit(solution)/shard_map/planes/pallas_call | solution.py:594
  8.4 0.0 collective-permute-done.from_low.a_2_.a_7_
  8.4 0.0 collective-permute-done.1.from_high.a_3_.a_8_
  8.4 0.1 corners.1
  8.5 2.3 %collective-permute-start.2 = (f32[168,128]{1,0:T(8,128)S(1)}, f32[168,128]{1,0:T(8,128)S(1)}, u32[]{:S(2)}, u32[]{:S(2)}) collective-permute-start(f32[168,128]{1,0:T(8,128)S(1)} %get-tuple-element.29), channel_id=1, source_target_pairs={{0,4},{4,8},{8,12},{12,16},{16,20},{20,24},{24,28},{28,0},{1,5},{5... | collective-permute-start | bytes 258056 | tf_op jit(solution)/shard_map/ppermute | solution.py:619
  10.8 3.1 %collective-permute-start.3 = (f32[168,128]{1,0:T(8,128)S(1)}, f32[168,128]{1,0:T(8,128)S(1)}, u32[]{:S(2)}, u32[]{:S(2)}) collective-permute-start(f32[168,128]{1,0:T(8,128)S(1)} %get-tuple-element.30), channel_id=1, source_target_pairs={{4,0},{8,4},{12,8},{16,12},{20,16},{24,20},{28,24},{0,28},{5,1},{9... | collective-permute-start | bytes 258056 | tf_op jit(solution)/shard_map/ppermute | solution.py:620
  13.9 3.3 %collective-permute-done.2.a_4_.a_9_ = f32[168,128]{1,0:T(8,128)S(1)} collective-permute-done((f32[168,128]{1,0:T(8,128)S(1)}, f32[168,128]{1,0:T(8,128)S(1)}, u32[]{:S(2)}, u32[]{:S(2)}) %collective-permute-start.2) | collective-permute-done | bytes 86048 | tf_op jit(solution)/shard_map/ppermute | solution.py:619
  17.3 0.3 collective-permute-done.3.a_5_.a_10_
  17.6 2.9 %solve.1 = (f32[5,320,128]{2,1,0:T(8,128)S(1)}, f32[328,128]{1,0:T(8,128)S(1)}, f32[32,128]{1,0:T(8,128)S(1)}) custom-call(f32[6,320,128]{2,1,0:T(8,128)S(1)} %get-tuple-element.23.a_0_, f32[320,128]{1,0:T(8,128)S(1)} %get-tuple-element.24.a_1_.a_5_, f32[72,128]{1,0:T(8,128)S(1)} %collective-permute-done.from_low.a_2_.a_7_, ...), custom_call_target="tpu_custom_call" | custom-call | tf_op jit(solution)/shard_map/solve/pallas_call | solution.py:622
  20.6 0.0 copy-start.9
  20.6 0.6 %copy-done.9 = f32[32,128]{1,0:T(8,128)} copy-done((f32[32,128]{1,0:T(8,128)}, f32[32,128]{1,0:T(8,128)S(1)}, u32[]{:S(2)}) %copy-start.9) | copy-done | bytes 16408
  21.2 4.9 %all-to-all-start = ((f32[32,1,128]{2,1,0:T(1,128)}), f32[32,1,128]{2,1,0:T(1,128)S(1)}, u32[]{:S(2)}, u32[]{:S(2)}) async-start(f32[32,1,128]{2,1,0:T(1,128)} %bitcast.11), calls=%async_computation | async-start | bytes 32768 | tf_op jit(solution)/shard_map/all_to_all | solution.py:643
  26.1 0.0 copy-start.8
  26.1 0.7 %copy-done.8 = s32[32,8]{0,1:T(8,128)S(1)} copy-done((s32[32,8]{0,1:T(8,128)S(1)}, s32[32,8]{0,1:T(8,128)}, u32[]{:S(2)}) %copy-start.8) | copy-done | bytes 1048
  26.8 3.7 %star.1 = (f32[4,320,128]{2,1,0:T(8,128)S(1)}, f32[4,320,128]{2,1,0:T(8,128)S(1)}, f32[4,320,128]{2,1,0:T(8,128)}) custom-call(f32[4,320,128]{2,1,0:T(8,128)S(1)} %get-tuple-element.34.a_0_, f32[4,320,128]{2,1,0:T(8,128)S(1)} %get-tuple-element.35.a_1_, f32[4,320,128]{2,1,0:T(8,128)S(1)} %copy-done, ...), custom_call_target="tpu_custom_call", output_to_operand_aliasing={{0}: (0, {}), {1}: (1, {})} | custom-call | flops 65536000 | bytes 3932160 | tf_op jit(solution)/shard_map/star/pallas_call | solution.py:645
  30.5 2.7 %all-to-all-done = f32[32,1,128]{2,1,0:T(1,128)S(1)} async-done(((f32[32,1,128]{2,1,0:T(1,128)}), f32[32,1,128]{2,1,0:T(1,128)S(1)}, u32[]{:S(2)}, u32[]{:S(2)}) %all-to-all-start) | async-done | bytes 16416 | tf_op jit(solution)/shard_map/all_to_all | solution.py:643
  33.2 2.0 %finish.1 = (f32[4,320,128]{2,1,0:T(8,128)}, f32[4,320,128]{2,1,0:T(8,128)}, f32[320,128]{1,0:T(8,128)}) custom-call(f32[32,128]{1,0:T(8,128)S(1)} %bitcast.6, f32[5,320,128]{2,1,0:T(8,128)S(1)} %get-tuple-element.32.a_1_, f32[328,128]{1,0:T(8,128)S(1)} %get-tuple-element.33.a_6_.a_2_, s32[320,128]{1,0:T(8,128)S(1)} %copy-done.1, s32[8,32]{1,0:T(8,128)S(1)} %bitcast.10, ...), custom_call_target="tpu_custom_call" | custom-call | tf_op jit(solution)/shard_map/finish/pallas_call | solution.py:658
Async XLA Ops:
  0.6 5.1 %copy-start = (f32[4,320,128]{2,1,0:T(8,128)S(1)}, f32[4,320,128]{2,1,0:T(8,128)}, u32[]{:S(2)}) copy-start(f32[4,320,128]{2,1,0:T(8,128)} %a_2_.5) | copy-start | bytes 1966084
  0.6 5.1 %copy-start.1 = (s32[320,128]{1,0:T(8,128)S(1)}, s32[320,128]{1,0:T(8,128)}, u32[]{:S(2)}) copy-start(s32[320,128]{1,0:T(8,128)} %a_3_.7) | copy-start | bytes 491524
  0.7 5.1 %copy-start.2 = (f32[4,320,128]{2,1,0:T(8,128)S(1)}, f32[4,320,128]{2,1,0:T(8,128)}, u32[]{:S(2)}) copy-start(f32[4,320,128]{2,1,0:T(8,128)} %a_0_.3) | copy-start | bytes 1966084
  0.7 5.1 %copy-start.3 = (f32[4,320,128]{2,1,0:T(8,128)S(1)}, f32[4,320,128]{2,1,0:T(8,128)}, u32[]{:S(2)}) copy-start(f32[4,320,128]{2,1,0:T(8,128)} %a_1_.3) | copy-start | bytes 1966084
  0.7 5.1 %copy-start.4 = (f32[320,128]{1,0:T(8,128)S(1)}, f32[320,128]{1,0:T(8,128)}, u32[]{:S(2)}) copy-start(f32[320,128]{1,0:T(8,128)} %a_3_.5) | copy-start | bytes 491524
  0.7 5.1 %copy-start.5 = (f32[320,128]{1,0:T(8,128)S(1)}, f32[320,128]{1,0:T(8,128)}, u32[]{:S(2)}) copy-start(f32[320,128]{1,0:T(8,128)} %a_4_.3) | copy-start | bytes 491524
  0.7 5.1 %copy-start.6 = (f32[320,128]{1,0:T(8,128)S(1)}, f32[320,128]{1,0:T(8,128)}, u32[]{:S(2)}) copy-start(f32[320,128]{1,0:T(8,128)} %a_5_.3) | copy-start | bytes 491524
  0.7 5.1 %copy-start.7 = (s32[32,8]{0,1:T(8,128)S(1)}, s32[32,8]{0,1:T(8,128)}, u32[]{:S(2)}) copy-start(s32[32,8]{0,1:T(8,128)} %param.17) | copy-start | bytes 3076
  3.2 5.2 %collective-permute-start = (f32[72,128]{1,0:T(8,128)}, f32[72,128]{1,0:T(8,128)S(1)}, u32[]{:S(2)}, u32[]{:S(2)}) collective-permute-start(f32[72,128]{1,0:T(8,128)} %get-tuple-element.25), channel_id=1, source_target_pairs={{0,1},{1,2},{2,3},{3,0},{4,5},{5,6},{6,7},{7,4},{8,9},{9,10},{10,1... | collective-permute-start | bytes 110600 | tf_op jit(solution)/shard_map/ppermute | solution.py:592
  3.8 4.7 %collective-permute-start.1 = (f32[72,128]{1,0:T(8,128)}, f32[72,128]{1,0:T(8,128)S(1)}, u32[]{:S(2)}, u32[]{:S(2)}) collective-permute-start(f32[72,128]{1,0:T(8,128)} %get-tuple-element.26), channel_id=1, source_target_pairs={{1,0},{2,1},{3,2},{0,3},{5,4},{6,5},{7,6},{4,7},{9,8},{10,9},{11,1... | collective-permute-start | bytes 110600 | tf_op jit(solution)/shard_map/ppermute | solution.py:593
  8.5 8.8 %collective-permute-start.2 = (f32[168,128]{1,0:T(8,128)S(1)}, f32[168,128]{1,0:T(8,128)S(1)}, u32[]{:S(2)}, u32[]{:S(2)}) collective-permute-start(f32[168,128]{1,0:T(8,128)S(1)} %get-tuple-element.29), channel_id=1, source_target_pairs={{0,4},{4,8},{8,12},{12,16},{16,20},{20,24},{24,28},{28,0},{1,5},{5... | collective-permute-start | bytes 258056 | tf_op jit(solution)/shard_map/ppermute | solution.py:619
  10.8 6.8 %collective-permute-start.3 = (f32[168,128]{1,0:T(8,128)S(1)}, f32[168,128]{1,0:T(8,128)S(1)}, u32[]{:S(2)}, u32[]{:S(2)}) collective-permute-start(f32[168,128]{1,0:T(8,128)S(1)} %get-tuple-element.30), channel_id=1, source_target_pairs={{4,0},{8,4},{12,8},{16,12},{20,16},{24,20},{28,24},{0,28},{5,1},{9... | collective-permute-start | bytes 258056 | tf_op jit(solution)/shard_map/ppermute | solution.py:620
  20.6 0.6 %copy-start.9 = (f32[32,128]{1,0:T(8,128)}, f32[32,128]{1,0:T(8,128)S(1)}, u32[]{:S(2)}) copy-start(f32[32,128]{1,0:T(8,128)S(1)} %get-tuple-element.31) | copy-start | bytes 49156
  21.2 12.0 %all-to-all-start = ((f32[32,1,128]{2,1,0:T(1,128)}), f32[32,1,128]{2,1,0:T(1,128)S(1)}, u32[]{:S(2)}, u32[]{:S(2)}) async-start(f32[32,1,128]{2,1,0:T(1,128)} %bitcast.11), calls=%async_computation | async-start | bytes 32768 | tf_op jit(solution)/shard_map/all_to_all | solution.py:643
  26.1 0.7 %copy-start.8 = (s32[32,8]{0,1:T(8,128)S(1)}, s32[32,8]{0,1:T(8,128)}, u32[]{:S(2)}) copy-start(s32[32,8]{0,1:T(8,128)} %param.16) | copy-start | bytes 3076

commit v3 on v2

--- a/solution.py
+++ b/solution.py
@@ -74,13 +74,18 @@
     return lax.axis_index("gx"), lax.axis_index("gy")
 
 
+def pick(axis, a, b):
+    odd = jnp.broadcast_to(lax.axis_index(axis) % 2, a.shape)
+    return jnp.where(odd == 0, a, b)
+
+
 def domain_at(tropic_ref, row_dev, col_dev, rows, row):
     block = row_dev * (rows // BY) + row // BY
     return jnp.where(tropic_ref[col_dev, block] >= 0, 1.0, 0.0).astype(f32)
 
 
 def rim_kernel(
-    rows, total_rows, u, v, t, p, depth, helm, land, tropic, low_out, high_out, s3, s2, si, sems
+    rows, total_rows, u, v, t, p, depth, helm, land, tropic, near_out, far_out, s3, s2, si, sems
 ):
     col_dev, row_dev = place()
     levels = u.shape[0]
@@ -96,7 +101,8 @@
         c.start()
     for c in copies:
         c.wait()
-    for side, (r0, out) in enumerate(((0, low_out), (rows - SUB, high_out))):
+    strips = []
+    for side, r0 in enumerate((0, rows - SUB)):
         domain = domain_at(tropic, row_dev, col_dev, rows, r0)
         us = [s3[side, 0, k] for k in range(levels)]
         vs = [s3[side, 1, k] for k in range(levels)]
@@ -104,16 +110,17 @@
             us, vs, s2[side, 0], s2[side, 1], s2[side, 2], si[side], domain,
             row_dev * rows + r0, total_rows,
         )
-        for i, plane in enumerate(planes):
-            out[pl.ds(SUB * i, SUB), :] = plane
         edge = 0 if side == 0 else SUB - 1
-        for i in range(3):
-            for k in range(levels):
-                n = SUB * NP + i * levels + k
-                out[n : n + 1, :] = s3[side, i, k, edge : edge + 1, :]
-        used = SUB * NP + 3 * levels
-        if used < out.shape[0]:
-            out[used:, :] = jnp.zeros((out.shape[0] - used, LANES), f32)
+        lines = [s3[side, i, k, edge : edge + 1, :] for i in range(3) for k in range(levels)]
+        spare = near_out.shape[0] - SUB * NP - len(lines)
+        lines.append(jnp.zeros((spare, LANES), f32))
+        strips.append(list(planes) + [jnp.concatenate(lines, 0)])
+    row = 0
+    for low, high in zip(*strips):
+        here = slice(row, row + low.shape[0])
+        near_out[here, :] = pick("gy", high, low)
+        far_out[here, :] = pick("gy", low, high)
+        row += low.shape[0]
 
 
 def pack_pair(low_fields, high_fields, extra_low, extra_high, to_west):
@@ -133,7 +140,8 @@
 
 
 def plane_kernel(
-    rows, total_rows, u, v, t, p, depth, helm, land, tropic, planes, wet, west, east, u_copy, v_copy
+    rows, total_rows, u, v, t, p, depth, helm, land, tropic, clinic, planes, wet, state, near, far,
+    u_copy, v_copy
 ):
     col_dev, row_dev = place()
     levels = u.shape[0]
@@ -153,6 +161,9 @@
         for i, plane in zip(OTHERS, range(NP - 1)):
             planes[plane, here, :] = out[i]
         wet[here, :] = out[WET]
+        block = row_dev * (rows // BY) + r // BY
+        active = clinic[col_dev, block].astype(f32)
+        state[here, :] = active + active * land[here, :].astype(f32)
         for k in range(levels):
             u_copy[k, here, :] = us[k]
             v_copy[k, here, :] = vs[k]
@@ -166,18 +177,26 @@
             low, extra_low = at(r)
             high, extra_high = at(r + half)
             here = pl.ds(pl.multiple_of(r, SUB), SUB)
-            west[here, :] = pack_pair(low, high, extra_low, extra_high, True)
-            east[here, :] = pack_pair(low, high, extra_low, extra_high, False)
+            west = pack_pair(low, high, extra_low, extra_high, True)
+            east = pack_pair(low, high, extra_low, extra_high, False)
+            near[here, :] = pick("gx", east, west)
+            far[here, :] = pick("gx", west, east)
         return carry
 
     lax.fori_loop(0, half // (SUB * unroll), body, 0)
 
 
-def corner_kernel(from_low, from_high, west_in, east_in, west, east):
-    low = [from_low[pl.ds(SUB * i, SUB), :] for i in range(NP)]
-    high = [from_high[pl.ds(SUB * i, SUB), :] for i in range(NP)]
-    west[...] = pack_pair(low, high, [], [], True)
-    east[...] = pack_pair(low, high, [], [], False)
+def corner_kernel(near_row, far_row, near_in, far_in, near, far):
+    low, high = [], []
+    for i in range(NP):
+        here = slice(SUB * i, SUB * i + SUB)
+        a, b = near_row[here, :], far_row[here, :]
+        low.append(pick("gy", b, a))
+        high.append(pick("gy", a, b))
+    west = pack_pair(low, high, [], [], True)
+    east = pack_pair(low, high, [], [], False)
+    near[...] = pick("gx", east, west)
+    far[...] = pick("gx", west, east)
 
 
 def shifted(c, h):
@@ -195,7 +214,7 @@
 
 
 def solve_kernel(
-    rows, planes, wet_in, from_low, from_high, from_west, from_east,
+    rows, planes, wet_in, near_row, far_row, near_col, far_col,
     basis, edge, partial, F, face_e, face_n, flow_e, flow_n, T, coef, diag,
 ):
     ext = rows + 2 * SUB
@@ -213,7 +232,8 @@
                 T[k, c, pl.ds(r, SUB), :] = zero8
 
     def unpack(dst, src, base):
-        e, w = from_east[src, :], from_west[src, :]
+        a, b = near_col[src, :], far_col[src, :]
+        e, w = pick("gx", a, b), pick("gx", b, a)
         lane = lane_of(e)
         for i in range(NP):
             lo = base + OFFSETS[i]
@@ -224,8 +244,9 @@
             F[i, 1, dst, :] = h
 
     for i in range(NP):
-        F[i, 0, pl.ds(SUB, SUB), :] = from_low[pl.ds(SUB * i, SUB), :]
-        F[i, 0, pl.ds(SUB + SUB + rows, SUB), :] = from_high[pl.ds(SUB * i, SUB), :]
+        a, b = near_row[pl.ds(SUB * i, SUB), :], far_row[pl.ds(SUB * i, SUB), :]
+        F[i, 0, pl.ds(SUB, SUB), :] = pick("gy", b, a)
+        F[i, 0, pl.ds(SUB + SUB + rows, SUB), :] = pick("gy", a, b)
         F[i, 0, pl.ds(2 * SUB, rows), :] = wet_in[...] if i == WET else planes[OTHERS.index(i)]
     unpack(pl.ds(SUB, SUB), pl.ds(half, SUB), 0)
     unpack(pl.ds(2 * SUB + rows, SUB), pl.ds(half, SUB), HALF)
@@ -418,7 +439,7 @@
 
 
 def star_kernel(
-    rows, total_rows, u, v, t, land, clinic, wet, edge, from_low, from_high, from_west, from_east,
+    rows, total_rows, u, v, t, state, wet, edge, near_row, far_row, near_col, far_col,
     u_out, v_out, t_out,
 ):
     col_dev, row_dev = place()
@@ -428,13 +449,12 @@
     for i, ref in enumerate((u, v, t)):
         for k in range(levels):
             n = SUB * NP + i * levels + k
-            below[i, k] = from_low[n : n + 1, :]
+            below[i, k] = pick("gy", far_row[n : n + 1, :], near_row[n : n + 1, :])
     for r in range(0, rows, BY):
-        block = row_dev * (rows // BY) + r // BY
-        active = clinic[col_dev, block].astype(f32)
         here = slice(r, r + BY)
-        keep = land[here, :].astype(f32) * active
-        rest = 1.0 - active
+        kind = state[here, :]
+        keep = jnp.where(kind > 1.5, 1.0, 0.0)
+        rest = jnp.where(kind < 0.5, 1.0, 0.0)
         h = wet[here, :]
         lane = lane_of(h)
         first, last = lane == 0, lane == LANES - 1
@@ -452,18 +472,21 @@
         coriolis = 0.2 + 0.6 * ((row.astype(f32) + 0.5) / total_rows)
         src = slice(r % half, r % half + BY)
         base = HALF * (r // half) + EDGE
+        a, b = near_col[src, :], far_col[src, :]
+        from_east, from_west = pick("gx", a, b), pick("gx", b, a)
         now = {(i, k): ref[k, here, :] for i, ref in enumerate((u, v, t)) for k in range(levels)}
 
         def around(ref, which, k):
             i = SUB * NP + which * levels + k
             a = now[which, k]
             lo = base + which * levels + k
-            e = jnp.where(last, roll(from_east[src, :], LANES - 1 - lo), roll(a, -1))
-            w = jnp.where(first, roll(from_west[src, :], -lo), roll(a, 1))
+            e = jnp.where(last, roll(from_east, LANES - 1 - lo), roll(a, -1))
+            w = jnp.where(first, roll(from_west, -lo), roll(a, 1))
             if r + BY < rows:
                 n = ref[k, r + 1 : r + BY + 1, :]
             else:
-                n = jnp.concatenate([a[1:], from_high[i : i + 1, :]], 0)
+                above = pick("gy", near_row[i : i + 1, :], far_row[i : i + 1, :])
+                n = jnp.concatenate([a[1:], above], 0)
             s = jnp.concatenate([below[which, k], a[:-1]], 0)
             return a, e, w, n, s
 
@@ -504,9 +527,8 @@
 
 
 def finish_kernel(
-    rows, parts, basis, edge, land, clinic, u, v, u_out, v_out, p_out
+    rows, parts, basis, edge, state, u, v, u_out, v_out, p_out
 ):
-    col_dev, row_dev = place()
     levels = u.shape[0]
     lane1 = lax.broadcasted_iota(jnp.int32, (1, LANES), 1)
     line = jnp.sum(parts[...], axis=0, keepdims=True)
@@ -532,8 +554,7 @@
     for r in range(0, rows, BY):
         here = slice(r, r + BY)
         p = p_out[here, :]
-        active = clinic[col_dev, row_dev * (rows // BY) + r // BY].astype(f32)
-        keep = land[here, :].astype(f32) * active
+        keep = jnp.where(state[here, :] > 1.5, 1.0, 0.0)
         side = jnp.sum(edge[here, :] * weights, axis=1, keepdims=True)
         east = jnp.where(lane_of(p) == LANES - 1, side, roll(p, -1))
         if r + BY < rows:
@@ -557,6 +578,13 @@
     return jax.ShapeDtypeStruct(dims, f32)
 
 
+def exchange(near, far, axis):
+    n = lax.axis_size(axis)
+    far = lax.ppermute(far, axis, [(i, (i + (1 if i % 2 else -1)) % n) for i in range(n)])
+    near = lax.ppermute(near, axis, [(i, i ^ 1) for i in range(n)])
+    return near, far
+
+
 def on_device(
     velocity_u, velocity_v, tracer, pressure_old, depth, helm, land_mask, clinic_map, tropic_map
 ):
@@ -564,6 +592,7 @@
     nx, ny = lax.axis_size("gx"), lax.axis_size("gy")
     total_rows = rows * ny
     assert cols == LANES == BX and rows % BY == 0 and rows % (2 * BY) == 0
+    assert nx % 2 == 0 and ny % 2 == 0
     assert EDGE + 3 * levels <= HALF and ITERS + 2 <= SUB
     half = rows // 2
     ext = rows + 2 * SUB
@@ -573,7 +602,8 @@
     def params(mib):
         return pltpu.CompilerParams(vmem_limit_bytes=mib << 20)
 
-    low, high = pl.pallas_call(
+    pinned = [pltpu.with_memory_space_constraint(f, pltpu.HBM) for f in fields[:7]]
+    near, far = pl.pallas_call(
         lambda *a: rim_kernel(rows, total_rows, *a),
         out_shape=(shape(strip, LANES), shape(strip, LANES)),
         in_specs=[HBM] * 7 + [SMEM],
@@ -584,27 +614,25 @@
             pltpu.VMEM((2, SUB, LANES), jnp.int32),
             pltpu.SemaphoreType.DMA((14,)),
         ],
-        compiler_params=params(58),
+        compiler_params=params(2),
         name="rim",
-    )(*fields)
-    up = [(i, (i + 1) % ny) for i in range(ny)]
-    down = [((i + 1) % ny, i) for i in range(ny)]
-    from_low = lax.ppermute(high, "gy", up)
-    from_high = lax.ppermute(low, "gy", down)
-    planes, wet, west, east, u_copy, v_copy = pl.pallas_call(
+    )(*pinned, pltpu.with_memory_space_constraint(tropic_map.T, pltpu.HBM))
+    near_row, far_row = exchange(near, far, "gy")
+    planes, wet, state, near, far, u_copy, v_copy = pl.pallas_call(
         lambda *a: plane_kernel(rows, total_rows, *a),
         out_shape=(
-            shape(NP - 1, rows, LANES), shape(rows, LANES), shape(half + SUB, LANES),
+            shape(NP - 1, rows, LANES), shape(rows, LANES), shape(rows, LANES),
+            shape(half + SUB, LANES),
             shape(half + SUB, LANES), shape(levels, rows, LANES), shape(levels, rows, LANES),
         ),
-        in_specs=[VMEM] * 7 + [SMEM],
-        out_specs=(VMEM,) * 6,
+        in_specs=[VMEM] * 7 + [SMEM] * 2,
+        out_specs=(VMEM,) * 7,
         compiler_params=params(6),
         name="planes",
-    )(*fields)
+    )(*fields, clinic_map.T)
     strip_spec = pl.BlockSpec((strip, LANES), lambda i: (0, 0))
     corner = pl.BlockSpec((SUB, LANES), lambda i: (half // SUB, 0))
-    west, east = pl.pallas_call(
+    near, far = pl.pallas_call(
         corner_kernel,
         grid=(1,),
         out_shape=(shape(half + SUB, LANES),) * 2,
@@ -613,11 +641,8 @@
         input_output_aliases={2: 0, 3: 1},
         compiler_params=params(2),
         name="corners",
-    )(from_low, from_high, west, east)
-    right = [(i, (i + 1) % nx) for i in range(nx)]
-    left = [((i + 1) % nx, i) for i in range(nx)]
-    from_west = lax.ppermute(east, "gx", right)
-    from_east = lax.ppermute(west, "gx", left)
+    )(near_row, far_row, near, far)
+    near_col, far_col = exchange(near, far, "gx")
     tall = ext + 2 * SUB
     basis, edge, partial = pl.pallas_call(
         lambda *a: solve_kernel(rows, *a),
@@ -639,30 +664,29 @@
         ],
         compiler_params=params(12),
         name="solve",
-    )(planes, wet, from_low, from_high, from_west, from_east)
+    )(planes, wet, near_row, far_row, near_col, far_col)
     parts = lax.all_to_all(partial, ("gx", "gy"), 0, 0, tiled=True)
     full = levels * rows * LANES
     u_base, v_base, t_new = pl.pallas_call(
         lambda *a: star_kernel(rows, total_rows, *a),
         out_shape=(shape(levels, rows, LANES),) * 3,
-        in_specs=[VMEM] * 4 + [SMEM] + [VMEM] * 6,
+        in_specs=[VMEM] * 10,
         out_specs=(VMEM,) * 3,
         input_output_aliases={0: 0, 1: 1},
         compiler_params=params(8),
         cost_estimate=pl.CostEstimate(flops=400 * full, bytes_accessed=24 * full, transcendentals=0),
         name="star",
     )(
-        u_copy, v_copy, tracer, land_mask, clinic_map.T, wet, edge, from_low, from_high,
-        from_west, from_east,
+        u_copy, v_copy, tracer, state, wet, edge, near_row, far_row, near_col, far_col
     )
     u_new, v_new, pressure = pl.pallas_call(
         lambda *a: finish_kernel(rows, *a),
         out_shape=(shape(levels, rows, LANES),) * 2 + (shape(rows, LANES),),
-        in_specs=[VMEM] * 4 + [SMEM] + [VMEM] * 2,
+        in_specs=[VMEM] * 6,
         out_specs=(VMEM,) * 3,
         compiler_params=params(4),
         name="finish",
-    )(parts, basis, edge, land_mask, clinic_map.T, u_base, v_base)
+    )(parts, basis, edge, state, u_base, v_base)
     return u_new, v_new, t_new, pressure
 
 

time: 35.5 us -> 33.8 us (0.952)
  Pallas kernels: 13.9 us -> 12.1 us
  waiting for transfers between devices: 6.39 us -> 7.64 us
  local copies, waits for them, and re-layouts: 1.32 us -> 0.64 us
  starting transfers between devices: 12.9 us -> 12.3 us
    all_to_all x1, waiting for transfers between devices: 2.72 us -> 4 us  [on_device(): parts = lax.all_to_all(partial, ('gx', 'gy'), 0, 0, tiled=True)]
    all_to_all x1, starting transfers between devices: 4.92 us -> 4.02 us  [on_device(): parts = lax.all_to_all(partial, ('gx', 'gy'), 0, 0, tiled=True)]
    unnamed x20, local copies, waits for them, and re-layouts: 1.32 us -> 0.64 us
    pallas_call x1, Pallas kernels: 2.49 us -> 1.86 us  [on_device(): pl.pallas_call(lambda *a: rim_kernel(rows, total_rows, *a), out_shape=(sh...]
    pallas_call x1, Pallas kernels: 2.04 us -> 1.44 us  [on_device(): pl.pallas_call(lambda *a: finish_kernel(rows, *a), out_shape=(shape(level...]
    pallas_call x1, Pallas kernels: 3.69 us -> 3.1 us  [on_device(): pl.pallas_call(lambda *a: star_kernel(rows, total_rows, *a), out_shape=(s...]
  transfers between devices with their start and end apart: 5 -> 5, of which waited for: 3 -> 3; matrix products, arithmetic and copies ran while one was open for 0% -> 0% of each run, Pallas kernels for 18% -> 17%
where the time goes in v3:
time: 33.8 us; the launch traced here: 33.5 us
  starting transfers between devices  12.3 us (36%)
  Pallas kernels  12.1 us (36%)
  waiting for transfers between devices  7.64 us (23%)
  between operations  0.81 us (2%)
  local copies, waits for them, and re-layouts  0.64 us (2%)
    ppermute x2, starting transfers between devices, exchange(): lax.ppermute(far, axis, [(i, (i + (1 if i % 2 else -1)) % n) for i in ran...  6.13 us
    all_to_all x1, starting transfers between devices, on_device(): parts = lax.all_to_all(partial, ('gx', 'gy'), 0, 0, tiled=True)  4.02 us
    all_to_all x1, waiting for transfers between devices, on_device(): parts = lax.all_to_all(partial, ('gx', 'gy'), 0, 0, tiled=True)  4 us
    ppermute x2, waiting for transfers between devices, exchange(): lax.ppermute(far, axis, [(i, (i + (1 if i % 2 else -1)) % n) for i in ran...  3.27 us
    pallas_call x1, Pallas kernels, on_device(): pl.pallas_call(lambda *a: star_kernel(rows, total_rows, *a), out_shape=(s...  3.1 us
    pallas_call x1, Pallas kernels, on_device(): pl.pallas_call(lambda *a: solve_kernel(rows, *a), out_shape=(shape(ITERS...  2.96 us
    pallas_call x1, Pallas kernels, on_device(): pl.pallas_call(lambda *a: plane_kernel(rows, total_rows, *a), out_shape=(...  2.68 us
    ppermute x2, starting transfers between devices, exchange(): near = lax.ppermute(near, axis, [(i, i ^ 1) for i in range(n)])  2.14 us
  transfers between devices with their start and end apart: 5, of which 3 were waited for; matrix products, arithmetic and copies ran while one was open for 0% of the time, Pallas kernels for 17%

profile of v3, /device:TPU:0, one launch (start us, length us, event | category | flops | bytes accessed | tf_op | source)
XLA Modules:
  0.0 33.5 jit_solution(8428217617501748061)
XLA Ops:
  0.6 0.0 copy-start
  0.6 0.0 copy-start.1
  0.7 0.0 copy-start.2
  0.7 0.0 copy-start.3
  0.7 0.0 copy-start.4
  0.7 0.0 copy-start.5
  0.7 0.0 copy-start.6
  0.7 0.0 copy-start.9
  0.7 1.9 %rim.1 = (f32[72,128]{1,0:T(8,128)S(1)}, f32[72,128]{1,0:T(8,128)S(1)}) custom-call(f32[4,320,128]{2,1,0:T(8,128)} %a_0_.3, f32[4,320,128]{2,1,0:T(8,128)} %a_1_.3, f32[4,320,128]{2,1,0:T(8,128)} %a_2_.5, f32[320,128]{1,0:T(8,128)} %a_3_.3, f32[320,128]{1,0:T(8,128)} %a_4_.3, f32[320,128]{1,0:T(8,128)} %a_5_.3, s32[320,128]{1,0:T(8,128)} %a_6_.3, ...), custom_call_target="tpu_custom_call" | custom-call | tf_op jit(solution)/shard_map/rim/pallas_call | solution.py:606
  2.6 0.0 copy-start.7
  2.6 0.6 %collective-permute-start = (f32[72,128]{1,0:T(8,128)S(1)}, f32[72,128]{1,0:T(8,128)S(1)}, u32[]{:S(2)}, u32[]{:S(2)}) collective-permute-start(f32[72,128]{1,0:T(8,128)S(1)} %get-tuple-element.26), channel_id=1, source_target_pairs={{0,1},{1,0},{2,3},{3,2},{4,5},{5,4},{6,7},{7,6},{8,9},{9,8},{10,11... | collective-permute-start | bytes 110600 | tf_op jit(solution)/shard_map/ppermute | solution.py:584
  3.2 2.6 %collective-permute-start.1 = (f32[72,128]{1,0:T(8,128)S(1)}, f32[72,128]{1,0:T(8,128)S(1)}, u32[]{:S(2)}, u32[]{:S(2)}) collective-permute-start(f32[72,128]{1,0:T(8,128)S(1)} %get-tuple-element.27), channel_id=1, source_target_pairs={{0,3},{1,2},{2,1},{3,0},{4,7},{5,6},{6,5},{7,4},{8,11},{9,10},{10,... | collective-permute-start | bytes 110600 | tf_op jit(solution)/shard_map/ppermute | solution.py:583
  5.7 0.0 copy-done
  5.7 0.0 copy-done.1
  5.8 0.0 copy-done.2
  5.8 0.0 copy-done.3
  5.8 0.0 copy-done.4
  5.8 0.0 copy-done.5
  5.8 0.0 copy-done.6
  5.8 0.0 copy-done.9
  5.8 0.0 copy-done.7
  5.8 2.7 %planes.1 = (f32[6,320,128]{2,1,0:T(8,128)S(1)}, f32[320,128]{1,0:T(8,128)S(1)}, f32[320,128]{1,0:T(8,128)S(1)}, f32[168,128]{1,0:T(8,128)S(1)}, f32[168,128]{1,...) custom-call(f32[4,320,128]{2,1,0:T(8,128)S(1)} %copy-done.1, f32[4,320,128]{2,1,0:T(8,128)S(1)} %copy-done.2, ...), custom_call_target="tpu_custom_call" | custom-call | tf_op jit(solution)/shard_map/planes/pallas_call | solution.py:621
  8.5 0.0 collective-permute-done.near_row.a_2_.a_6_
  8.5 0.0 collective-permute-done.1.far_row.a_3_.a_7_
  8.5 0.1 corners.1
  8.6 1.6 %collective-permute-start.2 = (f32[168,128]{1,0:T(8,128)S(1)}, f32[168,128]{1,0:T(8,128)S(1)}, u32[]{:S(2)}, u32[]{:S(2)}) collective-permute-start(f32[168,128]{1,0:T(8,128)S(1)} %get-tuple-element.30), channel_id=1, source_target_pairs={{0,4},{4,0},{8,12},{12,8},{16,20},{20,16},{24,28},{28,24},{1,5},{5... | collective-permute-start | bytes 258056 | tf_op jit(solution)/shard_map/ppermute | solution.py:584
  10.2 3.5 %collective-permute-start.3 = (f32[168,128]{1,0:T(8,128)S(1)}, f32[168,128]{1,0:T(8,128)S(1)}, u32[]{:S(2)}, u32[]{:S(2)}) collective-permute-start(f32[168,128]{1,0:T(8,128)S(1)} %get-tuple-element.31), channel_id=1, source_target_pairs={{0,28},{4,8},{8,4},{12,16},{16,12},{20,24},{24,20},{28,0},{1,29},{... | collective-permute-start | bytes 258056 | tf_op jit(solution)/shard_map/ppermute | solution.py:583
  13.7 0.4 %collective-permute-done.2.a_4_.a_8_ = f32[168,128]{1,0:T(8,128)S(1)} collective-permute-done((f32[168,128]{1,0:T(8,128)S(1)}, f32[168,128]{1,0:T(8,128)S(1)}, u32[]{:S(2)}, u32[]{:S(2)}) %collective-permute-start.2) | collective-permute-done | bytes 86048 | tf_op jit(solution)/shard_map/ppermute | solution.py:584
  14.1 3.3 %collective-permute-done.3.a_5_.a_9_ = f32[168,128]{1,0:T(8,128)S(1)} collective-permute-done((f32[168,128]{1,0:T(8,128)S(1)}, f32[168,128]{1,0:T(8,128)S(1)}, u32[]{:S(2)}, u32[]{:S(2)}) %collective-permute-start.3) | collective-permute-done | bytes 86048 | tf_op jit(solution)/shard_map/ppermute | solution.py:583
  17.4 3.0 %solve.1 = (f32[5,320,128]{2,1,0:T(8,128)S(1)}, f32[328,128]{1,0:T(8,128)S(1)}, f32[32,128]{1,0:T(8,128)S(1)}) custom-call(f32[6,320,128]{2,1,0:T(8,128)S(1)} %get-tuple-element.24.a_0_, f32[320,128]{1,0:T(8,128)S(1)} %get-tuple-element.25.a_1_.a_4_, f32[72,128]{1,0:T(8,128)S(1)} %collective-permute-done.near_row.a_2_.a_6_, ...), custom_call_target="tpu_custom_call" | custom-call | tf_op jit(solution)/shard_map/solve/pallas_call | solution.py:647
  20.4 0.0 copy-start.8
  20.4 0.6 %copy-done.8 = f32[32,128]{1,0:T(8,128)} copy-done((f32[32,128]{1,0:T(8,128)}, f32[32,128]{1,0:T(8,128)S(1)}, u32[]{:S(2)}) %copy-start.8) | copy-done | bytes 16408
  21.0 4.0 %all-to-all-start = ((f32[32,1,128]{2,1,0:T(1,128)}), f32[32,1,128]{2,1,0:T(1,128)S(1)}, u32[]{:S(2)}, u32[]{:S(2)}) async-start(f32[32,1,128]{2,1,0:T(1,128)} %bitcast.9), calls=%async_computation | async-start | bytes 32768 | tf_op jit(solution)/shard_map/all_to_all | solution.py:668
  25.0 3.1 %star.1 = (f32[4,320,128]{2,1,0:T(8,128)S(1)}, f32[4,320,128]{2,1,0:T(8,128)S(1)}, f32[4,320,128]{2,1,0:T(8,128)}) custom-call(f32[4,320,128]{2,1,0:T(8,128)S(1)} %get-tuple-element.36.a_0_, f32[4,320,128]{2,1,0:T(8,128)S(1)} %get-tuple-element.37.a_1_, f32[4,320,128]{2,1,0:T(8,128)S(1)} %copy-done, ...), custom_call_target="tpu_custom_call", output_to_operand_aliasing={{0}: (0, {}), {1}: (1, {})} | custom-call | flops 65536000 | bytes 3932160 | tf_op jit(solution)/shard_map/star/pallas_call | solution.py:670
  28.1 4.0 %all-to-all-done = f32[32,1,128]{2,1,0:T(1,128)S(1)} async-done(((f32[32,1,128]{2,1,0:T(1,128)}), f32[32,1,128]{2,1,0:T(1,128)S(1)}, u32[]{:S(2)}, u32[]{:S(2)}) %all-to-all-start) | async-done | bytes 16416 | tf_op jit(solution)/shard_map/all_to_all | solution.py:668
  32.1 1.4 %finish.1 = (f32[4,320,128]{2,1,0:T(8,128)}, f32[4,320,128]{2,1,0:T(8,128)}, f32[320,128]{1,0:T(8,128)}) custom-call(f32[32,128]{1,0:T(8,128)S(1)} %bitcast.6, f32[5,320,128]{2,1,0:T(8,128)S(1)} %get-tuple-element.33.a_1_, f32[328,128]{1,0:T(8,128)S(1)} %get-tuple-element.34.a_5_.a_2_, f32[320,128]{1,0:T(8,128)S(1)} %get-tuple-element.35.a_3_, ...), custom_call_target="tpu_custom_call" | custom-call | tf_op jit(solution)/shard_map/finish/pallas_call | solution.py:682
Async XLA Ops:
  0.6 5.1 %copy-start = (f32[4,320,128]{2,1,0:T(8,128)S(1)}, f32[4,320,128]{2,1,0:T(8,128)}, u32[]{:S(2)}) copy-start(f32[4,320,128]{2,1,0:T(8,128)} %a_2_.5) | copy-start | bytes 1966084
  0.6 5.1 %copy-start.1 = (f32[4,320,128]{2,1,0:T(8,128)S(1)}, f32[4,320,128]{2,1,0:T(8,128)}, u32[]{:S(2)}) copy-start(f32[4,320,128]{2,1,0:T(8,128)} %a_0_.3) | copy-start | bytes 1966084
  0.7 5.1 %copy-start.2 = (f32[4,320,128]{2,1,0:T(8,128)S(1)}, f32[4,320,128]{2,1,0:T(8,128)}, u32[]{:S(2)}) copy-start(f32[4,320,128]{2,1,0:T(8,128)} %a_1_.3) | copy-start | bytes 1966084
  0.7 5.1 %copy-start.3 = (f32[320,128]{1,0:T(8,128)S(1)}, f32[320,128]{1,0:T(8,128)}, u32[]{:S(2)}) copy-start(f32[320,128]{1,0:T(8,128)} %a_3_.3) | copy-start | bytes 491524
  0.7 5.1 %copy-start.4 = (f32[320,128]{1,0:T(8,128)S(1)}, f32[320,128]{1,0:T(8,128)}, u32[]{:S(2)}) copy-start(f32[320,128]{1,0:T(8,128)} %a_4_.3) | copy-start | bytes 491524
  0.7 5.1 %copy-start.5 = (f32[320,128]{1,0:T(8,128)S(1)}, f32[320,128]{1,0:T(8,128)}, u32[]{:S(2)}) copy-start(f32[320,128]{1,0:T(8,128)} %a_5_.3) | copy-start | bytes 491524
  0.7 5.1 %copy-start.6 = (s32[320,128]{1,0:T(8,128)S(1)}, s32[320,128]{1,0:T(8,128)}, u32[]{:S(2)}) copy-start(s32[320,128]{1,0:T(8,128)} %a_6_.3) | copy-start | bytes 491524
  0.7 5.1 %copy-start.9 = (s32[32,8]{0,1:T(8,128)S(1)}, s32[32,8]{0,1:T(8,128)}, u32[]{:S(2)}) copy-start(s32[32,8]{0,1:T(8,128)} %param.16) | copy-start | bytes 3076
  2.6 3.2 %copy-start.7 = (s32[32,8]{0,1:T(8,128)S(1)}, s32[32,8]{0,1:T(8,128)}, u32[]{:S(2)}) copy-start(s32[32,8]{0,1:T(8,128)} %param.17) | copy-start | bytes 3076
  2.6 5.9 %collective-permute-start = (f32[72,128]{1,0:T(8,128)S(1)}, f32[72,128]{1,0:T(8,128)S(1)}, u32[]{:S(2)}, u32[]{:S(2)}) collective-permute-start(f32[72,128]{1,0:T(8,128)S(1)} %get-tuple-element.26), channel_id=1, source_target_pairs={{0,1},{1,0},{2,3},{3,2},{4,5},{5,4},{6,7},{7,6},{8,9},{9,8},{10,11... | collective-permute-start | bytes 110600 | tf_op jit(solution)/shard_map/ppermute | solution.py:584
  3.2 5.3 %collective-permute-start.1 = (f32[72,128]{1,0:T(8,128)S(1)}, f32[72,128]{1,0:T(8,128)S(1)}, u32[]{:S(2)}, u32[]{:S(2)}) collective-permute-start(f32[72,128]{1,0:T(8,128)S(1)} %get-tuple-element.27), channel_id=1, source_target_pairs={{0,3},{1,2},{2,1},{3,0},{4,7},{5,6},{6,5},{7,4},{8,11},{9,10},{10,... | collective-permute-start | bytes 110600 | tf_op jit(solution)/shard_map/ppermute | solution.py:583
  8.6 5.5 %collective-permute-start.2 = (f32[168,128]{1,0:T(8,128)S(1)}, f32[168,128]{1,0:T(8,128)S(1)}, u32[]{:S(2)}, u32[]{:S(2)}) collective-permute-start(f32[168,128]{1,0:T(8,128)S(1)} %get-tuple-element.30), channel_id=1, source_target_pairs={{0,4},{4,0},{8,12},{12,8},{16,20},{20,16},{24,28},{28,24},{1,5},{5... | collective-permute-start | bytes 258056 | tf_op jit(solution)/shard_map/ppermute | solution.py:584
  10.2 7.2 %collective-permute-start.3 = (f32[168,128]{1,0:T(8,128)S(1)}, f32[168,128]{1,0:T(8,128)S(1)}, u32[]{:S(2)}, u32[]{:S(2)}) collective-permute-start(f32[168,128]{1,0:T(8,128)S(1)} %get-tuple-element.31), channel_id=1, source_target_pairs={{0,28},{4,8},{8,4},{12,16},{16,12},{20,24},{24,20},{28,0},{1,29},{... | collective-permute-start | bytes 258056 | tf_op jit(solution)/shard_map/ppermute | solution.py:583
  20.4 0.6 %copy-start.8 = (f32[32,128]{1,0:T(8,128)}, f32[32,128]{1,0:T(8,128)S(1)}, u32[]{:S(2)}) copy-start(f32[32,128]{1,0:T(8,128)S(1)} %get-tuple-element.32) | copy-start | bytes 49156
  21.0 11.1 %all-to-all-start = ((f32[32,1,128]{2,1,0:T(1,128)}), f32[32,1,128]{2,1,0:T(1,128)S(1)}, u32[]{:S(2)}, u32[]{:S(2)}) async-start(f32[32,1,128]{2,1,0:T(1,128)} %bitcast.9), calls=%async_computation | async-start | bytes 32768 | tf_op jit(solution)/shard_map/all_to_all | solution.py:668
